TPU v7x, 32 devices: a whole 2x2x4 slice. The times are simulated.
32 devices in a mesh: slab: 2 (over x), py: 4 (over y, core), px: 4 (over z).
Axes of the slice: x: 2, y: 2, z: 4, core: 2. Of those that a mesh axis runs over, the one named last changes fastest.
Arguments:
- state: bfloat16 [2, 3, 16, 1024, 1024], P(None, None, 'slab', ('py', 'px')), may hold values from -12 to 12
- shells: int32 [16, 1024, 1024], P('slab', ('py', 'px')), may hold values from 0 to 511
Outputs:
- restored: float32 [2, 3, 16, 1024, 1024], P(None, None, ('slab', 'py'), None, 'px')
- spectrum: float32 [512], replicated
All inputs are finite; a program needn't handle non-finite values.
Results may differ from a plain program's by a relative error of at most 0.0003.
Values may be sent and summed in bfloat16 or wider, within the bound.
No kernel may reach another device: no remote copies, remote signals or barrier semaphores. Data moves between devices by JAX's collectives and lax.ppermute only.
A program may use at most 128 MiB of HBM per device.

v0:
```python
import functools

import jax
import jax.numpy as jnp
from jax import lax
from jax.experimental import pallas as pl
from jax.experimental.pallas import tpu as pltpu
from jax.sharding import PartitionSpec as P


SHELLS = 512
LOW = 32
HIGH = SHELLS // LOW
LANES = 256
CUTS = (7, 10)
VMEM_LIMIT = 40 * 1024 * 1024
VMEM_FIRST = 56 * 1024 * 1024


def is_power(n):
    return n & (n - 1) == 0


def partner(i, step, n, back=False):
    if is_power(n):
        return i ^ step
    return (i - step + n) % n if back else (i + step) % n


def split3(x):
    a = x.astype(jnp.bfloat16)
    x = x - a.astype(jnp.float32)
    b = x.astype(jnp.bfloat16)
    return a, b, (x - b.astype(jnp.float32)).astype(jnp.bfloat16)


def whole_wait(ref, sem):
    pltpu.make_async_copy(ref, ref, sem).wait()


def pack_kernel(steps, sizes, planes, with_totals, *refs):
    (py_n, px_n), n = sizes, len(steps)
    refs = list(refs)
    state = refs.pop(0)
    totals = refs.pop(0) if with_totals else None
    outs, sems = refs[:n], refs[n]
    rows = state.shape[3]
    columns = outs[0].shape[1]
    me_y, me_x = lax.axis_index("py"), lax.axis_index("px")
    for k, (a, b, first, last, _) in enumerate(steps):
        to_y, to_x = partner(me_y, a, py_n), partner(me_x, b, px_n)
        across = pl.ds(pl.multiple_of(to_x * columns, columns), columns)
        for j in range(first, last):
            c, d, p = j // (3 * planes), j // planes % 3, j % planes
            pltpu.make_async_copy(
                state.at[c, d, to_y * planes + p, :, across],
                outs[k].at[pl.ds((j - first) * rows, rows), :],
                sems.at[k],
            ).start()
    if with_totals:
        t = totals[...]
        terms = split3(t) + (jnp.zeros_like(t).astype(jnp.bfloat16),)
        extra = jnp.concatenate([x.astype(jnp.float32) for x in terms], axis=0).astype(jnp.bfloat16)
        for k, (_, _, first, last, more) in enumerate(steps):
            if more:
                outs[k][pl.ds((last - first) * rows, 8), :] = extra
    for k, (_, _, first, last, _) in enumerate(steps):
        if first < last:
            whole_wait(outs[k].at[pl.ds(0, (last - first) * rows), :], sems.at[k])


def pack(state, totals, steps, sizes, planes):
    rows, columns = state.shape[3], state.shape[4] // sizes[1]
    shapes = [((l - f) * rows + (8 if more else 0), columns) for _, _, f, l, more in steps]
    vmem = pl.BlockSpec(memory_space=pltpu.VMEM)
    return pl.pallas_call(
        functools.partial(pack_kernel, steps, sizes, planes, totals is not None),
        out_shape=[jax.ShapeDtypeStruct(s, jnp.bfloat16) for s in shapes],
        in_specs=[pl.BlockSpec(memory_space=pltpu.HBM)] + ([vmem] if totals is not None else []),
        out_specs=[vmem] * len(steps),
        scratch_shapes=[pltpu.SemaphoreType.DMA((len(steps),))],
        compiler_params=pltpu.CompilerParams(
            vmem_limit_bytes=VMEM_FIRST if totals is None else VMEM_LIMIT
        ),
        cost_estimate=pl.CostEstimate(
            flops=0, bytes_accessed=sum(2 * r * c for r, c in shapes), transcendentals=0
        ),
        name="pack",
    )(state, *([totals] if totals is not None else []))


def unpack_kernel(steps, sizes, planes, with_base, scale, *refs):
    (py_n, px_n), n = sizes, len(steps)
    refs = list(refs)
    if with_base:
        refs.pop(0)
    mine = refs.pop(0) if scale is not None else None
    pieces = [refs.pop(0) for _ in range(n)]
    out = refs.pop(0)
    spectrum = refs.pop(0) if scale is not None else None
    wides, sems = refs[:n], refs[n]
    each = refs[n + 1] if scale is not None else None
    rows = out.shape[5]
    me_y, me_x = lax.axis_index("py"), lax.axis_index("px")
    for k, (a, b, first, last, more) in enumerate(steps):
        from_y, from_x = partner(me_y, a, py_n, True), partner(me_x, b, px_n, True)
        size = (last - first) * rows
        if first < last:
            wides[k][...] = pieces[k][pl.ds(0, size), :].astype(jnp.float32)
        for j in range(first, last):
            c, d, p = j // (3 * planes), j // planes % 3, j % planes
            pltpu.make_async_copy(
                wides[k].at[pl.ds((j - first) * rows, rows), :],
                out.at[c, d, p, from_y, from_x],
                sems.at[k],
            ).start()
        if more:
            extra = pieces[k][pl.ds(size, 8), :].astype(jnp.float32)
            each[from_y * px_n + from_x] = (extra[0:2] + extra[2:4]) + extra[4:6]
    if scale is not None:
        a, b, c = [x.astype(jnp.float32) for x in split3(mine[...])]
        each[me_y * px_n + me_x] = (a + b) + c
        total = each[0]
        for i in range(1, py_n * px_n):
            total = total + each[i]
        spectrum[...] = total * scale
    for k, (_, _, first, last, _) in enumerate(steps):
        if first < last:
            whole_wait(wides[k], sems.at[k])


def unpack(base, mine, pieces, steps, sizes, planes, rows, scale=None):
    py_n, px_n = sizes
    columns = pieces[0].shape[1]
    shape = (2, 3, planes, py_n, px_n, rows, columns)
    sizes_ = [(l - f) * rows for _, _, f, l, _ in steps]
    hbm, vmem = pl.BlockSpec(memory_space=pltpu.HBM), pl.BlockSpec(memory_space=pltpu.VMEM)
    args = ([base] if base is not None else []) + ([mine] if scale is not None else []) + list(pieces)
    specs = ([hbm] if base is not None else []) + [vmem] * (len(args) - (base is not None))
    outs, out_specs = [jax.ShapeDtypeStruct(shape, jnp.float32)], [hbm]
    extra = []
    if scale is not None:
        outs.append(jax.ShapeDtypeStruct(mine.shape, jnp.float32))
        out_specs.append(vmem)
        extra = [pltpu.VMEM((py_n * px_n,) + mine.shape, jnp.float32)]
    done = pl.pallas_call(
        functools.partial(unpack_kernel, steps, sizes, planes, base is not None, scale),
        out_shape=outs,
        in_specs=specs,
        out_specs=out_specs,
        scratch_shapes=[pltpu.VMEM((max(s, 8), columns), jnp.float32) for s in sizes_]
        + [pltpu.SemaphoreType.DMA((len(steps),))]
        + extra,
        input_output_aliases={0: 0} if base is not None else {},
        compiler_params=pltpu.CompilerParams(vmem_limit_bytes=VMEM_LIMIT),
        cost_estimate=pl.CostEstimate(
            flops=0, bytes_accessed=6 * columns * sum(sizes_), transcendentals=0
        ),
        name="unpack",
    )(*args)
    return done if scale is not None else done[0]


def bin_kernel(state, shells, out):
    rows = 8
    width = shells.shape[2]
    low_ids = lax.broadcasted_iota(jnp.int32, (LOW, width), 0)
    high_ids = lax.broadcasted_iota(jnp.int32, (HIGH, width), 0)

    @pl.when(pl.program_id(0) == 0)
    def _():
        out[...] = jnp.zeros_like(out)

    def body(i, total):
        r0 = pl.multiple_of(i * rows, rows)
        energy = jnp.zeros((rows, width), jnp.float32)
        for c in range(2):
            for d in range(3):
                v = state[c, d, 0, pl.ds(r0, rows), :].astype(jnp.float32)
                energy = energy + v * v
        labels = shells[0, pl.ds(r0, rows), :]
        low, high = labels % LOW, labels // LOW
        upper = energy.astype(jnp.bfloat16).astype(jnp.float32)
        lower = energy - upper
        lhs, rhs = [], []
        for r in range(rows):
            at_low = jnp.broadcast_to(low[r : r + 1], (LOW, width)) == low_ids
            at_high = jnp.broadcast_to(high[r : r + 1], (HIGH, width)) == high_ids
            up = jnp.where(at_high, jnp.broadcast_to(upper[r : r + 1], (HIGH, width)), 0.0)
            lo = jnp.where(at_high, jnp.broadcast_to(lower[r : r + 1], (HIGH, width)), 0.0)
            lhs.append(jnp.concatenate([up.astype(jnp.bfloat16), lo.astype(jnp.bfloat16)], axis=0))
            rhs.append(jnp.where(at_low, 1.0, 0.0).astype(jnp.bfloat16))
        part = lax.dot_general(
            jnp.concatenate(lhs, axis=1),
            jnp.concatenate(rhs, axis=1),
            (((1,), (1,)), ((), ())),
            preferred_element_type=jnp.float32,
        )
        return total + part

    total = lax.fori_loop(0, shells.shape[1] // rows, body, jnp.zeros((2 * HIGH, LOW), jnp.float32))
    out[...] += total[:HIGH] + total[HIGH:]


def bin_energy(state, shells):
    _, _, planes, rows, width = state.shape
    return pl.pallas_call(
        bin_kernel,
        grid=(planes,),
        out_shape=jax.ShapeDtypeStruct((HIGH, LOW), jnp.float32),
        in_specs=[
            pl.BlockSpec((2, 3, 1, rows, width), lambda i: (0, 0, i, 0, 0)),
            pl.BlockSpec((1, rows, width), lambda i: (i, 0, 0)),
        ],
        out_specs=pl.BlockSpec((HIGH, LOW), lambda i: (0, 0)),
        cost_estimate=pl.CostEstimate(
            flops=4 * HIGH * LOW * planes * rows * width,
            bytes_accessed=16 * planes * rows * width,
            transcendentals=0,
        ),
        compiler_params=pltpu.CompilerParams(vmem_limit_bytes=VMEM_FIRST),
        name="bins",
    )(state, shells)


def steps_of(state, shells):
    py_n, px_n, slab_n = lax.axis_size("py"), lax.axis_size("px"), lax.axis_size("slab")
    sizes = (py_n, px_n)
    _, _, planes_all, rows, columns = state.shape
    planes = planes_all // py_n
    blocks = 6 * planes

    def send(x, step):
        a, b = step[:2]
        pairs = [
            (y * px_n + x_, partner(y, a, py_n) * px_n + partner(x_, b, px_n))
            for y in range(py_n)
            for x_ in range(px_n)
        ]
        return lax.ppermute(x, ("py", "px"), pairs)

    cut1, cut2 = max(1, blocks * CUTS[0] // 12), max(2, blocks * CUTS[1] // 12)
    fars = [[(a, b) for a in range(py_n)] for b in reversed(range(px_n // 2, px_n))]
    nears = [[(a, b) for a in range(py_n) if (a, b) != (0, 0)] for b in reversed(range(px_n // 2))]
    far = [s for g in fars for s in g]
    near = [s for g in nears for s in g]

    def part(steps, first, last, more=False):
        return [s + (first, last, more) for s in steps]

    stages = [part(far[:1], 0, cut1), part(fars[0][1:], 0, cut1), part(nears[0], 0, blocks)]
    stages += [part(far[py_n:], 0, cut1)] + [part(g, 0, blocks) for g in nears[1:]]
    early = []
    for steps in stages:
        packed = pack(state, None, steps, sizes, planes)
        early.append((steps, [send(x, s) for x, s in zip(packed, steps)]))
    own = pack(state, None, [(0, 0, 0, blocks, False)], sizes, planes)
    totals = bin_energy(state, shells)
    totals = totals.reshape(SHELLS // LANES, LANES)
    shift = 1 if is_power(slab_n) else slab_n
    if not is_power(slab_n):
        totals = lax.psum(totals, "slab")
    while shift < slab_n:
        totals = totals + lax.ppermute(totals, "slab", [(i, partner(i, shift, slab_n)) for i in range(slab_n)])
        shift *= 2
    mid = part(far, cut1, cut2, True) + part(near, blocks, blocks, True)
    late = part(far, cut2, blocks)
    packed = pack(state, totals, mid + late, sizes, planes)
    got = [send(x, s) for x, s in zip(packed, mid + late)]
    modes = slab_n * py_n * px_n * planes_all * rows * columns

    out = unpack(None, None, own, [(0, 0, 0, blocks, False)], sizes, planes, rows)
    for steps, pieces in early:
        out = unpack(out, None, pieces, steps, sizes, planes, rows)
    out, spectrum = unpack(
        out, totals, got[: len(mid)], mid, sizes, planes, rows, scale=0.5 * SHELLS / modes
    )
    out = unpack(out, None, got[len(mid) :], late, sizes, planes, rows)
    restored = out.reshape(2, 3, planes, py_n * px_n * rows, columns // px_n)
    return (restored, spectrum.reshape(SHELLS))


def solution(mesh):
    return jax.shard_map(
        steps_of,
        mesh=mesh,
        in_specs=(P(None, None, "slab", ("py", "px"), None), P("slab", ("py", "px"), None)),
        out_specs=(P(None, None, ("slab", "py"), None, "px"), P()),
        check_vma=False,
    )
```

profile of v0, /device:TPU:0, one launch (start us, length us, event | category | flops | bytes accessed | tf_op | source)
XLA Modules:
  0.0 212.1 jit_solution(13190985401064856917)
XLA Ops:
  0.6 23.5 %bins.1 = f32[16,32]{1,0:T(8,128)} custom-call(bf16[2,3,8,64,1024]{4,3,2,1,0:T(8,128)(2,1)} %refs_0_.13, s32[8,64,1024]{2,1,0:T(8,128)} %shells.1), custom_call_target="tpu_custom_call" | custom-call | flops 1073741824 | bytes 8388608 | tf_op jit(solution)/shard_map/bins/pallas_call | solution.py:207
  24.2 0.8 reshape.13
  24.9 3.0 %collective-permute-start.15 = (f32[2,256]{1,0:T(2,128)S(1)}, f32[2,256]{1,0:T(2,128)S(1)}, u32[]{:S(2)}, u32[]{:S(2)}) collective-permute-start(f32[2,256]{1,0:T(2,128)S(1)} %reshape.13), channel_id=1, source_target_pairs={{0,16},{16,0},{1,17},{17,1},{2,18},{18,2},{3,19},{19,3},{4,20},{20... | collective-permute-start | bytes 6152 | tf_op jit(solution)/shard_map/ppermute | solution.py:264
  27.9 1.6 collective-permute-done.15
  29.5 2.8 %copy-done = bf16[2,3,8,64,1024]{4,3,2,1,0:T(8,128)(2,1)S(1)} copy-done((bf16[2,3,8,64,1024]{4,3,2,1,0:T(8,128)(2,1)S(1)}, bf16[2,3,8,64,1024]{4,3,2,1,0:T(8,128)(2,1)}, u32[]{:S(2)}) %copy-start) | copy-done | bytes 6291480
  32.3 0.6 pack.13
  32.8 2.2 %collective-permute-start.24 = (bf16[8,256]{1,0:T(8,128)(2,1)S(1)}, bf16[8,256]{1,0:T(8,128)(2,1)S(1)}, u32[]{:S(2)}, u32[]{:S(2)}) collective-permute-start(bf16[8,256]{1,0:T(8,128)(2,1)S(1)} %get-tuple-element.63), channel_id=1, source_target_pairs={{0,1},{1,0},{2,3},{3,2},{4,5},{5,4},{6,7},{7,6},{8,9},{9,8},{10,11... | collective-permute-start | bytes 12296 | tf_op jit(solution)/shard_map/ppermute | solution.py:240
  35.0 1.4 collective-permute-start.26
  36.4 1.3 collective-permute-start.27
  37.7 0.3 collective-permute-start.28
  38.0 3.4 %collective-permute-start.31 = (bf16[128,256]{1,0:T(8,128)(2,1)S(1)}, bf16[128,256]{1,0:T(8,128)(2,1)S(1)}, u32[]{:S(2)}, u32[]{:S(2)}) collective-permute-start(bf16[128,256]{1,0:T(8,128)(2,1)S(1)} %get-tuple-element.71), channel_id=1, source_target_pairs={{0,3},{1,2},{2,1},{3,0},{4,7},{5,6},{6,5},{7,4},{8,11},{9,10},{10,... | collective-permute-start | bytes 196616 | tf_op jit(solution)/shard_map/ppermute | solution.py:240
  41.4 0.2 collective-permute-start.32
  41.6 4.4 %collective-permute-start.33 = (bf16[128,256]{1,0:T(8,128)(2,1)S(1)}, bf16[128,256]{1,0:T(8,128)(2,1)S(1)}, u32[]{:S(2)}, u32[]{:S(2)}) collective-permute-start(bf16[128,256]{1,0:T(8,128)(2,1)S(1)} %get-tuple-element.73), channel_id=1, source_target_pairs={{0,11},{1,10},{2,9},{3,8},{4,15},{5,14},{6,13},{7,12},{8,3},{9,2},... | collective-permute-start | bytes 196616 | tf_op jit(solution)/shard_map/ppermute | solution.py:240
  46.0 0.5 collective-permute-start.29
  46.6 0.8 collective-permute-start.30
  47.4 2.8 %collective-permute-done.29.refs_15_ = bf16[8,256]{1,0:T(8,128)(2,1)S(1)} collective-permute-done((bf16[8,256]{1,0:T(8,128)(2,1)S(1)}, bf16[8,256]{1,0:T(8,128)(2,1)S(1)}, u32[]{:S(2)}, u32[]{:S(2)}) %collective-permute-start.29) | collective-permute-done | bytes 4128 | tf_op jit(solution)/shard_map/ppermute | solution.py:240
  50.2 1.8 collective-permute-start.17
  52.0 1.9 collective-permute-start.18
  53.9 4.3 %collective-permute-start.19 = (bf16[200,256]{1,0:T(8,128)(2,1)S(1)}, bf16[200,256]{1,0:T(8,128)(2,1)S(1)}, u32[]{:S(2)}, u32[]{:S(2)}) collective-permute-start(bf16[200,256]{1,0:T(8,128)(2,1)S(1)} %get-tuple-element.58), channel_id=1, source_target_pairs={{0,15},{1,14},{2,13},{3,12},{4,11},{5,10},{6,9},{7,8},{8,7},{9,6},... | collective-permute-start | bytes 307208 | tf_op jit(solution)/shard_map/ppermute | solution.py:240
  58.2 1.9 pack.9
  60.1 0.4 collective-permute-start.1
  60.5 1.7 collective-permute-start.2
  62.2 17.1 %collective-permute-start.21 = (bf16[200,256]{1,0:T(8,128)(2,1)S(1)}, bf16[200,256]{1,0:T(8,128)(2,1)S(1)}, u32[]{:S(2)}, u32[]{:S(2)}) collective-permute-start(bf16[200,256]{1,0:T(8,128)(2,1)S(1)} %get-tuple-element.60), channel_id=1, source_target_pairs={{0,6},{1,7},{2,4},{3,5},{4,2},{5,3},{6,0},{7,1},{8,14},{9,15},{10,... | collective-permute-start | bytes 307208 | tf_op jit(solution)/shard_map/ppermute | solution.py:240
  79.3 2.4 %collective-permute-start.22 = (bf16[200,256]{1,0:T(8,128)(2,1)S(1)}, bf16[200,256]{1,0:T(8,128)(2,1)S(1)}, u32[]{:S(2)}, u32[]{:S(2)}) collective-permute-start(bf16[200,256]{1,0:T(8,128)(2,1)S(1)} %get-tuple-element.61), channel_id=1, source_target_pairs={{0,10},{1,11},{2,8},{3,9},{4,14},{5,15},{6,12},{7,13},{8,2},{9,3},... | collective-permute-start | bytes 307208 | tf_op jit(solution)/shard_map/ppermute | solution.py:240
  81.7 0.9 collective-permute-done.20.refs_6_
  82.6 1.6 collective-permute-start.23
  84.2 1.5 pack.8
  85.8 14.5 %collective-permute-done.21.refs_7_ = bf16[200,256]{1,0:T(8,128)(2,1)S(1)} collective-permute-done((bf16[200,256]{1,0:T(8,128)(2,1)S(1)}, bf16[200,256]{1,0:T(8,128)(2,1)S(1)}, u32[]{:S(2)}, u32[]{:S(2)}) %collective-permute-start.21) | collective-permute-done | bytes 102432 | tf_op jit(solution)/shard_map/ppermute | solution.py:240
  100.3 4.3 %collective-permute-start.3 = (bf16[448,256]{1,0:T(8,128)(2,1)}, bf16[448,256]{1,0:T(8,128)(2,1)S(1)}, u32[]{:S(2)}, u32[]{:S(2)}) collective-permute-start(bf16[448,256]{1,0:T(8,128)(2,1)} %get-tuple-element.43), channel_id=1, source_target_pairs={{0,15},{1,14},{2,13},{3,12},{4,11},{5,10},{6,9},{7,8},{8,7},{9,6},... | collective-permute-start | bytes 688136 | tf_op jit(solution)/shard_map/ppermute | solution.py:240
  104.6 2.1 pack.11
  106.7 1.2 collective-permute-start
  107.9 2.5 %pack.10 = (bf16[768,256]{1,0:T(8,128)(2,1)}, bf16[768,256]{1,0:T(8,128)(2,1)}, bf16[768,256]{1,0:T(8,128)(2,1)}, bf16[768,256]{1,0:T(8,128)(2,1)}) custom-call(bf16[2,3,8,64,1024]{4,3,2,1,0:T(8,128)(2,1)} %refs_0_.13), custom_call_target="tpu_custom_call" | custom-call | bytes 1572864 | tf_op jit(solution)/shard_map/pack/pallas_call | solution.py:76
  110.4 3.0 %collective-permute-start.4 = (bf16[768,256]{1,0:T(8,128)(2,1)}, bf16[768,256]{1,0:T(8,128)(2,1)S(1)}, u32[]{:S(2)}, u32[]{:S(2)}) collective-permute-start(bf16[768,256]{1,0:T(8,128)(2,1)} %get-tuple-element.44), channel_id=1, source_target_pairs={{0,1},{1,0},{2,3},{3,2},{4,5},{5,4},{6,7},{7,6},{8,9},{9,8},{10,11... | collective-permute-start | bytes 1179656 | tf_op jit(solution)/shard_map/ppermute | solution.py:240
  113.4 11.7 %collective-permute-start.5 = (bf16[768,256]{1,0:T(8,128)(2,1)}, bf16[768,256]{1,0:T(8,128)(2,1)S(1)}, u32[]{:S(2)}, u32[]{:S(2)}) collective-permute-start(bf16[768,256]{1,0:T(8,128)(2,1)} %get-tuple-element.45), channel_id=1, source_target_pairs={{0,5},{1,4},{2,7},{3,6},{4,1},{5,0},{6,3},{7,2},{8,13},{9,12},{10,... | collective-permute-start | bytes 1179656 | tf_op jit(solution)/shard_map/ppermute | solution.py:240
  125.1 2.0 collective-permute-start.11
  127.0 4.9 %collective-permute-start.8 = (bf16[448,256]{1,0:T(8,128)(2,1)}, bf16[448,256]{1,0:T(8,128)(2,1)S(1)}, u32[]{:S(2)}, u32[]{:S(2)}) collective-permute-start(bf16[448,256]{1,0:T(8,128)(2,1)} %get-tuple-element.48), channel_id=1, source_target_pairs={{0,2},{1,3},{2,0},{3,1},{4,6},{5,7},{6,4},{7,5},{8,10},{9,11},{10,... | collective-permute-start | bytes 688136 | tf_op jit(solution)/shard_map/ppermute | solution.py:240
  132.0 4.2 %collective-permute-done.10.refs_3_ = bf16[448,256]{1,0:T(8,128)(2,1)S(1)} collective-permute-done((bf16[448,256]{1,0:T(8,128)(2,1)}, bf16[448,256]{1,0:T(8,128)(2,1)S(1)}, u32[]{:S(2)}, u32[]{:S(2)}) %collective-permute-start.10) | collective-permute-done | bytes 229408 | tf_op jit(solution)/shard_map/ppermute | solution.py:240
  136.1 2.3 %pack.12 = (bf16[768,256]{1,0:T(8,128)(2,1)}, bf16[768,256]{1,0:T(8,128)(2,1)}, bf16[768,256]{1,0:T(8,128)(2,1)}) custom-call(bf16[2,3,8,64,1024]{4,3,2,1,0:T(8,128)(2,1)} %refs_0_.13), custom_call_target="tpu_custom_call" | custom-call | bytes 1179648 | tf_op jit(solution)/shard_map/pack/pallas_call | solution.py:76
  138.4 3.1 %collective-permute-done.11.refs_4_ = bf16[448,256]{1,0:T(8,128)(2,1)S(1)} collective-permute-done((bf16[448,256]{1,0:T(8,128)(2,1)}, bf16[448,256]{1,0:T(8,128)(2,1)S(1)}, u32[]{:S(2)}, u32[]{:S(2)}) %collective-permute-start.11) | collective-permute-done | bytes 229408 | tf_op jit(solution)/shard_map/ppermute | solution.py:240
  141.6 11.3 %collective-permute-start.6 = (bf16[768,256]{1,0:T(8,128)(2,1)}, bf16[768,256]{1,0:T(8,128)(2,1)S(1)}, u32[]{:S(2)}, u32[]{:S(2)}) collective-permute-start(bf16[768,256]{1,0:T(8,128)(2,1)} %get-tuple-element.46), channel_id=1, source_target_pairs={{0,9},{1,8},{2,11},{3,10},{4,13},{5,12},{6,15},{7,14},{8,1},{9,0},... | collective-permute-start | bytes 1179656 | tf_op jit(solution)/shard_map/ppermute | solution.py:240
  152.9 6.1 %collective-permute-start.7 = (bf16[768,256]{1,0:T(8,128)(2,1)}, bf16[768,256]{1,0:T(8,128)(2,1)S(1)}, u32[]{:S(2)}, u32[]{:S(2)}) collective-permute-start(bf16[768,256]{1,0:T(8,128)(2,1)} %get-tuple-element.47), channel_id=1, source_target_pairs={{0,13},{1,12},{2,15},{3,14},{4,9},{5,8},{6,11},{7,10},{8,5},{9,4},... | collective-permute-start | bytes 1179656 | tf_op jit(solution)/shard_map/ppermute | solution.py:240
  159.0 4.8 %collective-permute-done.9.refs_2_ = bf16[448,256]{1,0:T(8,128)(2,1)S(1)} collective-permute-done((bf16[448,256]{1,0:T(8,128)(2,1)}, bf16[448,256]{1,0:T(8,128)(2,1)S(1)}, u32[]{:S(2)}, u32[]{:S(2)}) %collective-permute-start.9) | collective-permute-done | bytes 229408 | tf_op jit(solution)/shard_map/ppermute | solution.py:240
  163.8 0.5 collective-permute-start.12
  164.3 1.5 collective-permute-start.13
  165.9 5.5 %collective-permute-done.6.refs_3_ = bf16[768,256]{1,0:T(8,128)(2,1)S(1)} collective-permute-done((bf16[768,256]{1,0:T(8,128)(2,1)}, bf16[768,256]{1,0:T(8,128)(2,1)S(1)}, u32[]{:S(2)}, u32[]{:S(2)}) %collective-permute-start.6) | collective-permute-done | bytes 393248 | tf_op jit(solution)/shard_map/ppermute | solution.py:240
  171.3 4.4 %collective-permute-start.34 = (bf16[128,256]{1,0:T(8,128)(2,1)S(1)}, bf16[128,256]{1,0:T(8,128)(2,1)S(1)}, u32[]{:S(2)}, u32[]{:S(2)}) collective-permute-start(bf16[128,256]{1,0:T(8,128)(2,1)S(1)} %get-tuple-element.74), channel_id=1, source_target_pairs={{0,15},{1,14},{2,13},{3,12},{4,11},{5,10},{6,9},{7,8},{8,7},{9,6},... | collective-permute-start | bytes 196616 | tf_op jit(solution)/shard_map/ppermute | solution.py:240
  175.7 4.8 %collective-permute-done.7.refs_4_ = bf16[768,256]{1,0:T(8,128)(2,1)S(1)} collective-permute-done((bf16[768,256]{1,0:T(8,128)(2,1)}, bf16[768,256]{1,0:T(8,128)(2,1)S(1)}, u32[]{:S(2)}, u32[]{:S(2)}) %collective-permute-start.7) | collective-permute-done | bytes 393248 | tf_op jit(solution)/shard_map/ppermute | solution.py:240
  180.5 5.5 %collective-permute-start.35 = (bf16[128,256]{1,0:T(8,128)(2,1)S(1)}, bf16[128,256]{1,0:T(8,128)(2,1)S(1)}, u32[]{:S(2)}, u32[]{:S(2)}) collective-permute-start(bf16[128,256]{1,0:T(8,128)(2,1)S(1)} %get-tuple-element.75), channel_id=1, source_target_pairs={{0,2},{1,3},{2,0},{3,1},{4,6},{5,7},{6,4},{7,5},{8,10},{9,11},{10,... | collective-permute-start | bytes 196616 | tf_op jit(solution)/shard_map/ppermute | solution.py:240
  186.0 3.3 %collective-permute-done.13.refs_2_ = bf16[768,256]{1,0:T(8,128)(2,1)S(1)} collective-permute-done((bf16[768,256]{1,0:T(8,128)(2,1)}, bf16[768,256]{1,0:T(8,128)(2,1)S(1)}, u32[]{:S(2)}, u32[]{:S(2)}) %collective-permute-start.13) | collective-permute-done | bytes 393248 | tf_op jit(solution)/shard_map/ppermute | solution.py:240
  189.2 0.4 collective-permute-start.37
  189.7 9.2 %collective-permute-done.14.refs_3_ = bf16[768,256]{1,0:T(8,128)(2,1)S(1)} collective-permute-done((bf16[768,256]{1,0:T(8,128)(2,1)}, bf16[768,256]{1,0:T(8,128)(2,1)S(1)}, u32[]{:S(2)}, u32[]{:S(2)}) %collective-permute-start.14) | collective-permute-done | bytes 393248 | tf_op jit(solution)/shard_map/ppermute | solution.py:240
  198.9 0.2 collective-permute-start.38
  199.1 1.7 pack.7.refs_0_
  200.8 0.0 copy-start.1
  200.8 1.0 copy-done.1
  201.8 0.9 unpack.8.refs_0_
  202.8 0.8 unpack.9.refs_0_
  203.6 1.1 unpack.10.refs_0_
  204.7 1.7 unpack.11.refs_0_
  206.4 1.3 unpack.12.refs_0_
  207.7 1.4 unpack.13.refs_0_
  209.1 1.3 unpack.14
  210.4 0.6 copy.11
  211.0 1.0 unpack.15
  (37 shorter events, 0.1 us)
Async XLA Ops:
  24.9 4.5 %collective-permute-start.15 = (f32[2,256]{1,0:T(2,128)S(1)}, f32[2,256]{1,0:T(2,128)S(1)}, u32[]{:S(2)}, u32[]{:S(2)}) collective-permute-start(f32[2,256]{1,0:T(2,128)S(1)} %reshape.13), channel_id=1, source_target_pairs={{0,16},{16,0},{1,17},{17,1},{2,18},{18,2},{3,19},{19,3},{4,20},{20... | collective-permute-start | bytes 6152 | tf_op jit(solution)/shard_map/ppermute | solution.py:264
  29.5 2.8 %copy-start = (bf16[2,3,8,64,1024]{4,3,2,1,0:T(8,128)(2,1)S(1)}, bf16[2,3,8,64,1024]{4,3,2,1,0:T(8,128)(2,1)}, u32[]{:S(2)}) copy-start(bf16[2,3,8,64,1024]{4,3,2,1,0:T(8,128)(2,1)} %refs_0_.13) | copy-start | bytes 18874372
  32.8 5.2 %collective-permute-start.24 = (bf16[8,256]{1,0:T(8,128)(2,1)S(1)}, bf16[8,256]{1,0:T(8,128)(2,1)S(1)}, u32[]{:S(2)}, u32[]{:S(2)}) collective-permute-start(bf16[8,256]{1,0:T(8,128)(2,1)S(1)} %get-tuple-element.63), channel_id=1, source_target_pairs={{0,1},{1,0},{2,3},{3,2},{4,5},{5,4},{6,7},{7,6},{8,9},{9,8},{10,11... | collective-permute-start | bytes 12296 | tf_op jit(solution)/shard_map/ppermute | solution.py:240
  35.0 6.4 %collective-permute-start.25 = (bf16[8,256]{1,0:T(8,128)(2,1)S(1)}, bf16[8,256]{1,0:T(8,128)(2,1)S(1)}, u32[]{:S(2)}, u32[]{:S(2)}) collective-permute-start(bf16[8,256]{1,0:T(8,128)(2,1)S(1)} %get-tuple-element.64), channel_id=1, source_target_pairs={{0,5},{1,4},{2,7},{3,6},{4,1},{5,0},{6,3},{7,2},{8,13},{9,12},{10,... | collective-permute-start | bytes 12296 | tf_op jit(solution)/shard_map/ppermute | solution.py:240
  35.0 6.6 %collective-permute-start.26 = (bf16[8,256]{1,0:T(8,128)(2,1)S(1)}, bf16[8,256]{1,0:T(8,128)(2,1)S(1)}, u32[]{:S(2)}, u32[]{:S(2)}) collective-permute-start(bf16[8,256]{1,0:T(8,128)(2,1)S(1)} %get-tuple-element.65), channel_id=1, source_target_pairs={{0,9},{1,8},{2,11},{3,10},{4,13},{5,12},{6,15},{7,14},{8,1},{9,0},... | collective-permute-start | bytes 12296 | tf_op jit(solution)/shard_map/ppermute | solution.py:240
  36.4 9.6 %collective-permute-start.27 = (bf16[8,256]{1,0:T(8,128)(2,1)S(1)}, bf16[8,256]{1,0:T(8,128)(2,1)S(1)}, u32[]{:S(2)}, u32[]{:S(2)}) collective-permute-start(bf16[8,256]{1,0:T(8,128)(2,1)S(1)} %get-tuple-element.66), channel_id=1, source_target_pairs={{0,13},{1,12},{2,15},{3,14},{4,9},{5,8},{6,11},{7,10},{8,5},{9,4},... | collective-permute-start | bytes 12296 | tf_op jit(solution)/shard_map/ppermute | solution.py:240
  37.7 8.8 %collective-permute-start.28 = (bf16[8,256]{1,0:T(8,128)(2,1)S(1)}, bf16[8,256]{1,0:T(8,128)(2,1)S(1)}, u32[]{:S(2)}, u32[]{:S(2)}) collective-permute-start(bf16[8,256]{1,0:T(8,128)(2,1)S(1)} %get-tuple-element.67), channel_id=1, source_target_pairs={{0,4},{1,5},{2,6},{3,7},{4,0},{5,1},{6,2},{7,3},{8,12},{9,13},{10,... | collective-permute-start | bytes 12296 | tf_op jit(solution)/shard_map/ppermute | solution.py:240
  38.0 14.0 %collective-permute-start.31 = (bf16[128,256]{1,0:T(8,128)(2,1)S(1)}, bf16[128,256]{1,0:T(8,128)(2,1)S(1)}, u32[]{:S(2)}, u32[]{:S(2)}) collective-permute-start(bf16[128,256]{1,0:T(8,128)(2,1)S(1)} %get-tuple-element.71), channel_id=1, source_target_pairs={{0,3},{1,2},{2,1},{3,0},{4,7},{5,6},{6,5},{7,4},{8,11},{9,10},{10,... | collective-permute-start | bytes 196616 | tf_op jit(solution)/shard_map/ppermute | solution.py:240
  41.4 12.5 %collective-permute-start.32 = (bf16[128,256]{1,0:T(8,128)(2,1)S(1)}, bf16[128,256]{1,0:T(8,128)(2,1)S(1)}, u32[]{:S(2)}, u32[]{:S(2)}) collective-permute-start(bf16[128,256]{1,0:T(8,128)(2,1)S(1)} %get-tuple-element.72), channel_id=1, source_target_pairs={{0,7},{1,6},{2,5},{3,4},{4,3},{5,2},{6,1},{7,0},{8,15},{9,14},{10,... | collective-permute-start | bytes 196616 | tf_op jit(solution)/shard_map/ppermute | solution.py:240
  41.6 16.6 %collective-permute-start.33 = (bf16[128,256]{1,0:T(8,128)(2,1)S(1)}, bf16[128,256]{1,0:T(8,128)(2,1)S(1)}, u32[]{:S(2)}, u32[]{:S(2)}) collective-permute-start(bf16[128,256]{1,0:T(8,128)(2,1)S(1)} %get-tuple-element.73), channel_id=1, source_target_pairs={{0,11},{1,10},{2,9},{3,8},{4,15},{5,14},{6,13},{7,12},{8,3},{9,2},... | collective-permute-start | bytes 196616 | tf_op jit(solution)/shard_map/ppermute | solution.py:240
  46.0 4.1 %collective-permute-start.29 = (bf16[8,256]{1,0:T(8,128)(2,1)S(1)}, bf16[8,256]{1,0:T(8,128)(2,1)S(1)}, u32[]{:S(2)}, u32[]{:S(2)}) collective-permute-start(bf16[8,256]{1,0:T(8,128)(2,1)S(1)} %get-tuple-element.68), channel_id=1, source_target_pairs={{0,8},{1,9},{2,10},{3,11},{4,12},{5,13},{6,14},{7,15},{8,0},{9,1},... | collective-permute-start | bytes 12296 | tf_op jit(solution)/shard_map/ppermute | solution.py:240
  46.6 3.6 %collective-permute-start.30 = (bf16[8,256]{1,0:T(8,128)(2,1)S(1)}, bf16[8,256]{1,0:T(8,128)(2,1)S(1)}, u32[]{:S(2)}, u32[]{:S(2)}) collective-permute-start(bf16[8,256]{1,0:T(8,128)(2,1)S(1)} %get-tuple-element.69), channel_id=1, source_target_pairs={{0,12},{1,13},{2,14},{3,15},{4,8},{5,9},{6,10},{7,11},{8,4},{9,5},... | collective-permute-start | bytes 12296 | tf_op jit(solution)/shard_map/ppermute | solution.py:240
  50.2 10.0 %collective-permute-start.16 = (bf16[200,256]{1,0:T(8,128)(2,1)S(1)}, bf16[200,256]{1,0:T(8,128)(2,1)S(1)}, u32[]{:S(2)}, u32[]{:S(2)}) collective-permute-start(bf16[200,256]{1,0:T(8,128)(2,1)S(1)} %get-tuple-element.55), channel_id=1, source_target_pairs={{0,3},{1,2},{2,1},{3,0},{4,7},{5,6},{6,5},{7,4},{8,11},{9,10},{10,... | collective-permute-start | bytes 307208 | tf_op jit(solution)/shard_map/ppermute | solution.py:240
  50.2 10.4 %collective-permute-start.17 = (bf16[200,256]{1,0:T(8,128)(2,1)S(1)}, bf16[200,256]{1,0:T(8,128)(2,1)S(1)}, u32[]{:S(2)}, u32[]{:S(2)}) collective-permute-start(bf16[200,256]{1,0:T(8,128)(2,1)S(1)} %get-tuple-element.56), channel_id=1, source_target_pairs={{0,7},{1,6},{2,5},{3,4},{4,3},{5,2},{6,1},{7,0},{8,15},{9,14},{10,... | collective-permute-start | bytes 307208 | tf_op jit(solution)/shard_map/ppermute | solution.py:240
  52.0 10.3 %collective-permute-start.18 = (bf16[200,256]{1,0:T(8,128)(2,1)S(1)}, bf16[200,256]{1,0:T(8,128)(2,1)S(1)}, u32[]{:S(2)}, u32[]{:S(2)}) collective-permute-start(bf16[200,256]{1,0:T(8,128)(2,1)S(1)} %get-tuple-element.57), channel_id=1, source_target_pairs={{0,11},{1,10},{2,9},{3,8},{4,15},{5,14},{6,13},{7,12},{8,3},{9,2},... | collective-permute-start | bytes 307208 | tf_op jit(solution)/shard_map/ppermute | solution.py:240
  53.9 25.4 %collective-permute-start.19 = (bf16[200,256]{1,0:T(8,128)(2,1)S(1)}, bf16[200,256]{1,0:T(8,128)(2,1)S(1)}, u32[]{:S(2)}, u32[]{:S(2)}) collective-permute-start(bf16[200,256]{1,0:T(8,128)(2,1)S(1)} %get-tuple-element.58), channel_id=1, source_target_pairs={{0,15},{1,14},{2,13},{3,12},{4,11},{5,10},{6,9},{7,8},{8,7},{9,6},... | collective-permute-start | bytes 307208 | tf_op jit(solution)/shard_map/ppermute | solution.py:240
  58.2 24.4 %collective-permute-start.20 = (bf16[200,256]{1,0:T(8,128)(2,1)S(1)}, bf16[200,256]{1,0:T(8,128)(2,1)S(1)}, u32[]{:S(2)}, u32[]{:S(2)}) collective-permute-start(bf16[200,256]{1,0:T(8,128)(2,1)S(1)} %get-tuple-element.59), channel_id=1, source_target_pairs={{0,2},{1,3},{2,0},{3,1},{4,6},{5,7},{6,4},{7,5},{8,10},{9,11},{10,... | collective-permute-start | bytes 307208 | tf_op jit(solution)/shard_map/ppermute | solution.py:240
  60.1 50.3 %collective-permute-start.1 = (bf16[448,256]{1,0:T(8,128)(2,1)}, bf16[448,256]{1,0:T(8,128)(2,1)S(1)}, u32[]{:S(2)}, u32[]{:S(2)}) collective-permute-start(bf16[448,256]{1,0:T(8,128)(2,1)} %get-tuple-element.41), channel_id=1, source_target_pairs={{0,7},{1,6},{2,5},{3,4},{4,3},{5,2},{6,1},{7,0},{8,15},{9,14},{10,... | collective-permute-start | bytes 688136 | tf_op jit(solution)/shard_map/ppermute | solution.py:240
  60.5 52.8 %collective-permute-start.2 = (bf16[448,256]{1,0:T(8,128)(2,1)}, bf16[448,256]{1,0:T(8,128)(2,1)S(1)}, u32[]{:S(2)}, u32[]{:S(2)}) collective-permute-start(bf16[448,256]{1,0:T(8,128)(2,1)} %get-tuple-element.42), channel_id=1, source_target_pairs={{0,11},{1,10},{2,9},{3,8},{4,15},{5,14},{6,13},{7,12},{8,3},{9,2},... | collective-permute-start | bytes 688136 | tf_op jit(solution)/shard_map/ppermute | solution.py:240
  62.2 38.0 %collective-permute-start.21 = (bf16[200,256]{1,0:T(8,128)(2,1)S(1)}, bf16[200,256]{1,0:T(8,128)(2,1)S(1)}, u32[]{:S(2)}, u32[]{:S(2)}) collective-permute-start(bf16[200,256]{1,0:T(8,128)(2,1)S(1)} %get-tuple-element.60), channel_id=1, source_target_pairs={{0,6},{1,7},{2,4},{3,5},{4,2},{5,3},{6,0},{7,1},{8,14},{9,15},{10,... | collective-permute-start | bytes 307208 | tf_op jit(solution)/shard_map/ppermute | solution.py:240
  79.3 27.4 %collective-permute-start.22 = (bf16[200,256]{1,0:T(8,128)(2,1)S(1)}, bf16[200,256]{1,0:T(8,128)(2,1)S(1)}, u32[]{:S(2)}, u32[]{:S(2)}) collective-permute-start(bf16[200,256]{1,0:T(8,128)(2,1)S(1)} %get-tuple-element.61), channel_id=1, source_target_pairs={{0,10},{1,11},{2,8},{3,9},{4,14},{5,15},{6,12},{7,13},{8,2},{9,3},... | collective-permute-start | bytes 307208 | tf_op jit(solution)/shard_map/ppermute | solution.py:240
  82.6 25.3 %collective-permute-start.23 = (bf16[200,256]{1,0:T(8,128)(2,1)S(1)}, bf16[200,256]{1,0:T(8,128)(2,1)S(1)}, u32[]{:S(2)}, u32[]{:S(2)}) collective-permute-start(bf16[200,256]{1,0:T(8,128)(2,1)S(1)} %get-tuple-element.62), channel_id=1, source_target_pairs={{0,14},{1,15},{2,12},{3,13},{4,10},{5,11},{6,8},{7,9},{8,6},{9,7},... | collective-permute-start | bytes 307208 | tf_op jit(solution)/shard_map/ppermute | solution.py:240
  100.3 24.8 %collective-permute-start.3 = (bf16[448,256]{1,0:T(8,128)(2,1)}, bf16[448,256]{1,0:T(8,128)(2,1)S(1)}, u32[]{:S(2)}, u32[]{:S(2)}) collective-permute-start(bf16[448,256]{1,0:T(8,128)(2,1)} %get-tuple-element.43), channel_id=1, source_target_pairs={{0,15},{1,14},{2,13},{3,12},{4,11},{5,10},{6,9},{7,8},{8,7},{9,6},... | collective-permute-start | bytes 688136 | tf_op jit(solution)/shard_map/ppermute | solution.py:240
  106.7 20.3 %collective-permute-start = (bf16[448,256]{1,0:T(8,128)(2,1)}, bf16[448,256]{1,0:T(8,128)(2,1)S(1)}, u32[]{:S(2)}, u32[]{:S(2)}) collective-permute-start(bf16[448,256]{1,0:T(8,128)(2,1)} %pack.8), channel_id=1, source_target_pairs={{0,3},{1,2},{2,1},{3,0},{4,7},{5,6},{6,5},{7,4},{8,11},{9,10},{10,... | collective-permute-start | bytes 688136 | tf_op jit(solution)/shard_map/ppermute | solution.py:240
  107.9 28.3 %collective-permute-start.10 = (bf16[448,256]{1,0:T(8,128)(2,1)}, bf16[448,256]{1,0:T(8,128)(2,1)S(1)}, u32[]{:S(2)}, u32[]{:S(2)}) collective-permute-start(bf16[448,256]{1,0:T(8,128)(2,1)} %get-tuple-element.50), channel_id=1, source_target_pairs={{0,10},{1,11},{2,8},{3,9},{4,14},{5,15},{6,12},{7,13},{8,2},{9,3},... | collective-permute-start | bytes 688136 | tf_op jit(solution)/shard_map/ppermute | solution.py:240
  110.4 53.9 %collective-permute-start.4 = (bf16[768,256]{1,0:T(8,128)(2,1)}, bf16[768,256]{1,0:T(8,128)(2,1)S(1)}, u32[]{:S(2)}, u32[]{:S(2)}) collective-permute-start(bf16[768,256]{1,0:T(8,128)(2,1)} %get-tuple-element.44), channel_id=1, source_target_pairs={{0,1},{1,0},{2,3},{3,2},{4,5},{5,4},{6,7},{7,6},{8,9},{9,8},{10,11... | collective-permute-start | bytes 1179656 | tf_op jit(solution)/shard_map/ppermute | solution.py:240
  113.4 52.5 %collective-permute-start.5 = (bf16[768,256]{1,0:T(8,128)(2,1)}, bf16[768,256]{1,0:T(8,128)(2,1)S(1)}, u32[]{:S(2)}, u32[]{:S(2)}) collective-permute-start(bf16[768,256]{1,0:T(8,128)(2,1)} %get-tuple-element.45), channel_id=1, source_target_pairs={{0,5},{1,4},{2,7},{3,6},{4,1},{5,0},{6,3},{7,2},{8,13},{9,12},{10,... | collective-permute-start | bytes 1179656 | tf_op jit(solution)/shard_map/ppermute | solution.py:240
  125.1 16.5 %collective-permute-start.11 = (bf16[448,256]{1,0:T(8,128)(2,1)}, bf16[448,256]{1,0:T(8,128)(2,1)S(1)}, u32[]{:S(2)}, u32[]{:S(2)}) collective-permute-start(bf16[448,256]{1,0:T(8,128)(2,1)} %get-tuple-element.51), channel_id=1, source_target_pairs={{0,14},{1,15},{2,12},{3,13},{4,10},{5,11},{6,8},{7,9},{8,6},{9,7},... | collective-permute-start | bytes 688136 | tf_op jit(solution)/shard_map/ppermute | solution.py:240
  127.0 25.9 %collective-permute-start.8 = (bf16[448,256]{1,0:T(8,128)(2,1)}, bf16[448,256]{1,0:T(8,128)(2,1)S(1)}, u32[]{:S(2)}, u32[]{:S(2)}) collective-permute-start(bf16[448,256]{1,0:T(8,128)(2,1)} %get-tuple-element.48), channel_id=1, source_target_pairs={{0,2},{1,3},{2,0},{3,1},{4,6},{5,7},{6,4},{7,5},{8,10},{9,11},{10,... | collective-permute-start | bytes 688136 | tf_op jit(solution)/shard_map/ppermute | solution.py:240
  136.1 27.7 %collective-permute-start.9 = (bf16[448,256]{1,0:T(8,128)(2,1)}, bf16[448,256]{1,0:T(8,128)(2,1)S(1)}, u32[]{:S(2)}, u32[]{:S(2)}) collective-permute-start(bf16[448,256]{1,0:T(8,128)(2,1)} %get-tuple-element.49), channel_id=1, source_target_pairs={{0,6},{1,7},{2,4},{3,5},{4,2},{5,3},{6,0},{7,1},{8,14},{9,15},{10,... | collective-permute-start | bytes 688136 | tf_op jit(solution)/shard_map/ppermute | solution.py:240
  141.6 29.7 %collective-permute-start.6 = (bf16[768,256]{1,0:T(8,128)(2,1)}, bf16[768,256]{1,0:T(8,128)(2,1)S(1)}, u32[]{:S(2)}, u32[]{:S(2)}) collective-permute-start(bf16[768,256]{1,0:T(8,128)(2,1)} %get-tuple-element.46), channel_id=1, source_target_pairs={{0,9},{1,8},{2,11},{3,10},{4,13},{5,12},{6,15},{7,14},{8,1},{9,0},... | collective-permute-start | bytes 1179656 | tf_op jit(solution)/shard_map/ppermute | solution.py:240
  152.9 27.6 %collective-permute-start.7 = (bf16[768,256]{1,0:T(8,128)(2,1)}, bf16[768,256]{1,0:T(8,128)(2,1)S(1)}, u32[]{:S(2)}, u32[]{:S(2)}) collective-permute-start(bf16[768,256]{1,0:T(8,128)(2,1)} %get-tuple-element.47), channel_id=1, source_target_pairs={{0,13},{1,12},{2,15},{3,14},{4,9},{5,8},{6,11},{7,10},{8,5},{9,4},... | collective-permute-start | bytes 1179656 | tf_op jit(solution)/shard_map/ppermute | solution.py:240
  163.8 22.2 %collective-permute-start.12 = (bf16[768,256]{1,0:T(8,128)(2,1)}, bf16[768,256]{1,0:T(8,128)(2,1)S(1)}, u32[]{:S(2)}, u32[]{:S(2)}) collective-permute-start(bf16[768,256]{1,0:T(8,128)(2,1)} %get-tuple-element.52), channel_id=1, source_target_pairs={{0,4},{1,5},{2,6},{3,7},{4,0},{5,1},{6,2},{7,3},{8,12},{9,13},{10,... | collective-permute-start | bytes 1179656 | tf_op jit(solution)/shard_map/ppermute | solution.py:240
  164.3 24.9 %collective-permute-start.13 = (bf16[768,256]{1,0:T(8,128)(2,1)}, bf16[768,256]{1,0:T(8,128)(2,1)S(1)}, u32[]{:S(2)}, u32[]{:S(2)}) collective-permute-start(bf16[768,256]{1,0:T(8,128)(2,1)} %get-tuple-element.53), channel_id=1, source_target_pairs={{0,8},{1,9},{2,10},{3,11},{4,12},{5,13},{6,14},{7,15},{8,0},{9,1},... | collective-permute-start | bytes 1179656 | tf_op jit(solution)/shard_map/ppermute | solution.py:240
  165.9 33.0 %collective-permute-start.14 = (bf16[768,256]{1,0:T(8,128)(2,1)}, bf16[768,256]{1,0:T(8,128)(2,1)S(1)}, u32[]{:S(2)}, u32[]{:S(2)}) collective-permute-start(bf16[768,256]{1,0:T(8,128)(2,1)} %get-tuple-element.54), channel_id=1, source_target_pairs={{0,12},{1,13},{2,14},{3,15},{4,8},{5,9},{6,10},{7,11},{8,4},{9,5},... | collective-permute-start | bytes 1179656 | tf_op jit(solution)/shard_map/ppermute | solution.py:240
  171.3 39.7 %collective-permute-start.34 = (bf16[128,256]{1,0:T(8,128)(2,1)S(1)}, bf16[128,256]{1,0:T(8,128)(2,1)S(1)}, u32[]{:S(2)}, u32[]{:S(2)}) collective-permute-start(bf16[128,256]{1,0:T(8,128)(2,1)S(1)} %get-tuple-element.74), channel_id=1, source_target_pairs={{0,15},{1,14},{2,13},{3,12},{4,11},{5,10},{6,9},{7,8},{8,7},{9,6},... | collective-permute-start | bytes 196616 | tf_op jit(solution)/shard_map/ppermute | solution.py:240
  180.5 30.5 %collective-permute-start.35 = (bf16[128,256]{1,0:T(8,128)(2,1)S(1)}, bf16[128,256]{1,0:T(8,128)(2,1)S(1)}, u32[]{:S(2)}, u32[]{:S(2)}) collective-permute-start(bf16[128,256]{1,0:T(8,128)(2,1)S(1)} %get-tuple-element.75), channel_id=1, source_target_pairs={{0,2},{1,3},{2,0},{3,1},{4,6},{5,7},{6,4},{7,5},{8,10},{9,11},{10,... | collective-permute-start | bytes 196616 | tf_op jit(solution)/shard_map/ppermute | solution.py:240
  186.0 25.0 %collective-permute-start.36 = (bf16[128,256]{1,0:T(8,128)(2,1)S(1)}, bf16[128,256]{1,0:T(8,128)(2,1)S(1)}, u32[]{:S(2)}, u32[]{:S(2)}) collective-permute-start(bf16[128,256]{1,0:T(8,128)(2,1)S(1)} %get-tuple-element.76), channel_id=1, source_target_pairs={{0,6},{1,7},{2,4},{3,5},{4,2},{5,3},{6,0},{7,1},{8,14},{9,15},{10,... | collective-permute-start | bytes 196616 | tf_op jit(solution)/shard_map/ppermute | solution.py:240
  189.2 21.8 %collective-permute-start.37 = (bf16[128,256]{1,0:T(8,128)(2,1)S(1)}, bf16[128,256]{1,0:T(8,128)(2,1)S(1)}, u32[]{:S(2)}, u32[]{:S(2)}) collective-permute-start(bf16[128,256]{1,0:T(8,128)(2,1)S(1)} %get-tuple-element.77), channel_id=1, source_target_pairs={{0,10},{1,11},{2,8},{3,9},{4,14},{5,15},{6,12},{7,13},{8,2},{9,3},... | collective-permute-start | bytes 196616 | tf_op jit(solution)/shard_map/ppermute | solution.py:240
  198.9 12.1 %collective-permute-start.38 = (bf16[128,256]{1,0:T(8,128)(2,1)S(1)}, bf16[128,256]{1,0:T(8,128)(2,1)S(1)}, u32[]{:S(2)}, u32[]{:S(2)}) collective-permute-start(bf16[128,256]{1,0:T(8,128)(2,1)S(1)} %get-tuple-element.78), channel_id=1, source_target_pairs={{0,14},{1,15},{2,12},{3,13},{4,10},{5,11},{6,8},{7,9},{8,6},{9,7},... | collective-permute-start | bytes 196616 | tf_op jit(solution)/shard_map/ppermute | solution.py:240
  200.8 1.0 copy-start.1
where the time goes:
time: 216 us; the launch traced here: 212 us
  starting transfers between devices  106 us (49%)
  waiting for transfers between devices  54.6 us (25%)
  Pallas kernels  45.7 us (21%)
  local copies, waits for them, and re-layouts  5.13 us (2%)
    ppermute x38, starting transfers between devices, send(): return lax.ppermute(x, ('py', 'px'), pairs)  103 us
    ppermute x38, waiting for transfers between devices, send(): return lax.ppermute(x, ('py', 'px'), pairs)  53 us
    pallas_call x1, Pallas kernels, bin_energy(): pl.pallas_call(bin_kernel, grid=(planes,), out_shape=jax.ShapeDtypeStruct...  23.5 us
    pallas_call x7, Pallas kernels, pack(): pl.pallas_call(functools.partial(pack_kernel, steps, sizes, planes, total...  12.6 us
    pallas_call x8, Pallas kernels, unpack(): pl.pallas_call(functools.partial(unpack_kernel, steps, sizes, planes, bas...  9.57 us
    unnamed x5, local copies, waits for them, and re-layouts  4.36 us
  transfers between devices with their start and end apart: 39, of which 11 were waited for; matrix products, arithmetic and copies ran while one was open for 0% of the time, Pallas kernels for 10%

commit v1 on v0

--- a/solution.py
+++ b/solution.py
@@ -25,6 +25,10 @@
     if is_power(n):
         return i ^ step
     return (i - step + n) % n if back else (i + step) % n
+
+
+def joined(n):
+    return 2 if n > 1 and is_power(n) else 1
 
 
 def split3(x):
@@ -101,6 +105,7 @@
     wides, sems = refs[:n], refs[n]
     each = refs[n + 1] if scale is not None else None
     rows = out.shape[5]
+    joint = joined(py_n)
     me_y, me_x = lax.axis_index("py"), lax.axis_index("px")
     for k, (a, b, first, last, more) in enumerate(steps):
         from_y, from_x = partner(me_y, a, py_n, True), partner(me_x, b, px_n, True)
@@ -116,12 +121,12 @@
             ).start()
         if more:
             extra = pieces[k][pl.ds(size, 8), :].astype(jnp.float32)
-            each[from_y * px_n + from_x] = (extra[0:2] + extra[2:4]) + extra[4:6]
+            each[from_y // joint * px_n + from_x] = (extra[0:2] + extra[2:4]) + extra[4:6]
     if scale is not None:
         a, b, c = [x.astype(jnp.float32) for x in split3(mine[...])]
-        each[me_y * px_n + me_x] = (a + b) + c
+        each[me_y // joint * px_n + me_x] = (a + b) + c
         total = each[0]
-        for i in range(1, py_n * px_n):
+        for i in range(1, py_n // joint * px_n):
             total = total + each[i]
         spectrum[...] = total * scale
     for k, (_, _, first, last, _) in enumerate(steps):
@@ -142,7 +147,7 @@
     if scale is not None:
         outs.append(jax.ShapeDtypeStruct(mine.shape, jnp.float32))
         out_specs.append(vmem)
-        extra = [pltpu.VMEM((py_n * px_n,) + mine.shape, jnp.float32)]
+        extra = [pltpu.VMEM((py_n // joined(py_n) * px_n,) + mine.shape, jnp.float32)]
     done = pl.pallas_call(
         functools.partial(unpack_kernel, steps, sizes, planes, base is not None, scale),
         out_shape=outs,
@@ -257,14 +262,17 @@
     own = pack(state, None, [(0, 0, 0, blocks, False)], sizes, planes)
     totals = bin_energy(state, shells)
     totals = totals.reshape(SHELLS // LANES, LANES)
-    shift = 1 if is_power(slab_n) else slab_n
-    if not is_power(slab_n):
-        totals = lax.psum(totals, "slab")
-    while shift < slab_n:
-        totals = totals + lax.ppermute(totals, "slab", [(i, partner(i, shift, slab_n)) for i in range(slab_n)])
-        shift *= 2
-    mid = part(far, cut1, cut2, True) + part(near, blocks, blocks, True)
-    late = part(far, cut2, blocks)
+    joint = joined(py_n)
+    for axis, n, bits in (("slab", slab_n, slab_n.bit_length() - 1), ("py", py_n, joint - 1)):
+        if axis == "slab" and not is_power(n):
+            totals = lax.psum(totals, axis)
+            continue
+        for bit in range(bits):
+            pairs = [(i, i ^ (1 << bit)) for i in range(n)]
+            totals = totals + lax.ppermute(totals, axis, pairs)
+    mid = [s + (cut1, cut2, s[0] % joint == 0) for s in far]
+    mid += part([s for s in near if s[0] % joint == 0], blocks, blocks, True)
+    late = part([(a, b) for b in range(px_n // 2, px_n) for a in [*range(py_n // 2, py_n), *range(py_n // 2)]], cut2, blocks)
     packed = pack(state, totals, mid + late, sizes, planes)
     got = [send(x, s) for x, s in zip(packed, mid + late)]
     modes = slab_n * py_n * px_n * planes_all * rows * columns

time: 216 us -> 214 us (level); the launches traced: 212 us -> 214 us
  waiting for transfers between devices: 54.6 us -> 106 us
  starting transfers between devices: 106 us -> 55.8 us
    ppermute x38 -> x34, waiting for transfers between devices: 53 us -> 104 us  [send(): return lax.ppermute(x, ('py', 'px'), pairs)]
    ppermute x38 -> x34, starting transfers between devices: 103 us -> 52.8 us  [send(): return lax.ppermute(x, ('py', 'px'), pairs)]
  transfers between devices with their start and end apart: 39 -> 36, of which waited for: 11 -> 17; matrix products, arithmetic and copies ran while one was open for 0% -> 0% of each run, Pallas kernels for 10% -> 10%
where the time goes in v1:
time: 214 us
  waiting for transfers between devices  106 us (50%)
  starting transfers between devices  55.8 us (26%)
  Pallas kernels  45.7 us (21%)
  local copies, waits for them, and re-layouts  5.13 us (2%)
    ppermute x34, waiting for transfers between devices, send(): return lax.ppermute(x, ('py', 'px'), pairs)  104 us
    ppermute x34, starting transfers between devices, send(): return lax.ppermute(x, ('py', 'px'), pairs)  52.8 us
    pallas_call x1, Pallas kernels, bin_energy(): pl.pallas_call(bin_kernel, grid=(planes,), out_shape=jax.ShapeDtypeStruct...  23.5 us
    pallas_call x7, Pallas kernels, pack(): pl.pallas_call(functools.partial(pack_kernel, steps, sizes, planes, total...  12.6 us
    pallas_call x8, Pallas kernels, unpack(): pl.pallas_call(functools.partial(unpack_kernel, steps, sizes, planes, bas...  9.54 us
    unnamed x5, local copies, waits for them, and re-layouts  4.36 us
  transfers between devices with their start and end apart: 36, of which 17 were waited for; matrix products, arithmetic and copies ran while one was open for 0% of the time, Pallas kernels for 10%

profile of v1, /device:TPU:0, one launch (start us, length us, event | category | flops | bytes accessed | tf_op | source)
XLA Modules:
  0.0 213.7 jit_solution(6807494290586040720)
XLA Ops:
  0.6 23.5 %bins.1 = f32[16,32]{1,0:T(8,128)} custom-call(bf16[2,3,8,64,1024]{4,3,2,1,0:T(8,128)(2,1)} %refs_0_.13, s32[8,64,1024]{2,1,0:T(8,128)} %shells.1), custom_call_target="tpu_custom_call" | custom-call | flops 1073741824 | bytes 8388608 | tf_op jit(solution)/shard_map/bins/pallas_call | solution.py:212
  24.2 0.8 reshape.13
  24.9 3.0 %collective-permute-start.15 = (f32[2,256]{1,0:T(2,128)S(1)}, f32[2,256]{1,0:T(2,128)S(1)}, u32[]{:S(2)}, u32[]{:S(2)}) collective-permute-start(f32[2,256]{1,0:T(2,128)S(1)} %reshape.13), channel_id=1, source_target_pairs={{0,16},{16,0},{1,17},{17,1},{2,18},{18,2},{3,19},{19,3},{4,20},{20... | collective-permute-start | bytes 6152 | tf_op jit(solution)/shard_map/ppermute | solution.py:272
  27.9 1.6 collective-permute-done.15
  29.5 1.2 collective-permute-done.16
  30.6 2.8 %copy-done = bf16[2,3,8,64,1024]{4,3,2,1,0:T(8,128)(2,1)S(1)} copy-done((bf16[2,3,8,64,1024]{4,3,2,1,0:T(8,128)(2,1)S(1)}, bf16[2,3,8,64,1024]{4,3,2,1,0:T(8,128)(2,1)}, u32[]{:S(2)}) %copy-start) | copy-done | bytes 6291480
  33.4 0.5 pack.13
  33.9 4.1 %collective-permute-start.28 = (bf16[128,256]{1,0:T(8,128)(2,1)S(1)}, bf16[128,256]{1,0:T(8,128)(2,1)S(1)}, u32[]{:S(2)}, u32[]{:S(2)}) collective-permute-start(bf16[128,256]{1,0:T(8,128)(2,1)S(1)} %get-tuple-element.63), channel_id=1, source_target_pairs={{0,10},{1,11},{2,8},{3,9},{4,14},{5,15},{6,12},{7,13},{8,2},{9,3},... | collective-permute-start | bytes 196616 | tf_op jit(solution)/shard_map/ppermute | solution.py:245
  38.1 1.6 collective-permute-start.25
  39.7 0.0 collective-permute-start.29
  39.7 2.1 collective-permute-start.30
  41.7 1.4 collective-permute-start.26
  43.1 0.0 collective-permute-done.25.refs_10_
  43.1 0.5 collective-permute-start.27
  43.7 2.6 %collective-permute-done.26.refs_11_ = bf16[8,256]{1,0:T(8,128)(2,1)S(1)} collective-permute-done((bf16[8,256]{1,0:T(8,128)(2,1)S(1)}, bf16[8,256]{1,0:T(8,128)(2,1)S(1)}, u32[]{:S(2)}, u32[]{:S(2)}) %collective-permute-start.26) | collective-permute-done | bytes 4128 | tf_op jit(solution)/shard_map/ppermute | solution.py:245
  46.2 0.5 collective-permute-done.27.refs_12_
  46.8 4.4 %collective-permute-start.20 = (bf16[192,256]{1,0:T(8,128)(2,1)S(1)}, bf16[192,256]{1,0:T(8,128)(2,1)S(1)}, u32[]{:S(2)}, u32[]{:S(2)}) collective-permute-start(bf16[192,256]{1,0:T(8,128)(2,1)S(1)} %get-tuple-element.54), channel_id=1, source_target_pairs={{0,15},{1,14},{2,13},{3,12},{4,11},{5,10},{6,9},{7,8},{8,7},{9,6},... | collective-permute-start | bytes 294920 | tf_op jit(solution)/shard_map/ppermute | solution.py:245
  51.2 0.3 collective-permute-start.17
  51.4 2.6 %collective-permute-start.24 = (bf16[192,256]{1,0:T(8,128)(2,1)S(1)}, bf16[192,256]{1,0:T(8,128)(2,1)S(1)}, u32[]{:S(2)}, u32[]{:S(2)}) collective-permute-start(bf16[192,256]{1,0:T(8,128)(2,1)S(1)} %get-tuple-element.58), channel_id=1, source_target_pairs={{0,14},{1,15},{2,12},{3,13},{4,10},{5,11},{6,8},{7,9},{8,6},{9,7},... | collective-permute-start | bytes 294920 | tf_op jit(solution)/shard_map/ppermute | solution.py:245
  54.1 1.9 pack.9
  56.0 2.3 %collective-permute-start.1 = (bf16[448,256]{1,0:T(8,128)(2,1)}, bf16[448,256]{1,0:T(8,128)(2,1)S(1)}, u32[]{:S(2)}, u32[]{:S(2)}) collective-permute-start(bf16[448,256]{1,0:T(8,128)(2,1)} %get-tuple-element.37), channel_id=1, source_target_pairs={{0,7},{1,6},{2,5},{3,4},{4,3},{5,2},{6,1},{7,0},{8,15},{9,14},{10,... | collective-permute-start | bytes 688136 | tf_op jit(solution)/shard_map/ppermute | solution.py:245
  58.3 2.3 %collective-permute-start.2 = (bf16[448,256]{1,0:T(8,128)(2,1)}, bf16[448,256]{1,0:T(8,128)(2,1)S(1)}, u32[]{:S(2)}, u32[]{:S(2)}) collective-permute-start(bf16[448,256]{1,0:T(8,128)(2,1)} %get-tuple-element.38), channel_id=1, source_target_pairs={{0,11},{1,10},{2,9},{3,8},{4,15},{5,14},{6,13},{7,12},{8,3},{9,2},... | collective-permute-start | bytes 688136 | tf_op jit(solution)/shard_map/ppermute | solution.py:245
  60.6 18.5 %collective-permute-done.22.refs_7_ = bf16[192,256]{1,0:T(8,128)(2,1)S(1)} collective-permute-done((bf16[192,256]{1,0:T(8,128)(2,1)S(1)}, bf16[192,256]{1,0:T(8,128)(2,1)S(1)}, u32[]{:S(2)}, u32[]{:S(2)}) %collective-permute-start.22) | collective-permute-done | bytes 98336 | tf_op jit(solution)/shard_map/ppermute | solution.py:245
  79.1 1.0 collective-permute-start.19
  80.2 1.0 collective-permute-done.24.refs_9_
  81.2 3.9 %collective-permute-start.23 = (bf16[200,256]{1,0:T(8,128)(2,1)S(1)}, bf16[200,256]{1,0:T(8,128)(2,1)S(1)}, u32[]{:S(2)}, u32[]{:S(2)}) collective-permute-start(bf16[200,256]{1,0:T(8,128)(2,1)S(1)} %get-tuple-element.57), channel_id=1, source_target_pairs={{0,10},{1,11},{2,8},{3,9},{4,14},{5,15},{6,12},{7,13},{8,2},{9,3},... | collective-permute-start | bytes 307208 | tf_op jit(solution)/shard_map/ppermute | solution.py:245
  85.1 1.5 pack.8
  86.6 1.0 collective-permute-done.19.refs_4_
  87.6 2.1 pack.11
  89.8 17.0 %collective-permute-done.21.refs_6_ = bf16[200,256]{1,0:T(8,128)(2,1)S(1)} collective-permute-done((bf16[200,256]{1,0:T(8,128)(2,1)S(1)}, bf16[200,256]{1,0:T(8,128)(2,1)S(1)}, u32[]{:S(2)}, u32[]{:S(2)}) %collective-permute-start.21) | collective-permute-done | bytes 102432 | tf_op jit(solution)/shard_map/ppermute | solution.py:245
  106.8 1.7 collective-permute-start
  108.5 0.4 collective-permute-done.23.refs_8_
  108.9 0.8 collective-permute-start.10
  109.7 2.5 %pack.10 = (bf16[768,256]{1,0:T(8,128)(2,1)}, bf16[768,256]{1,0:T(8,128)(2,1)}, bf16[768,256]{1,0:T(8,128)(2,1)}, bf16[768,256]{1,0:T(8,128)(2,1)}) custom-call(bf16[2,3,8,64,1024]{4,3,2,1,0:T(8,128)(2,1)} %refs_0_.13), custom_call_target="tpu_custom_call" | custom-call | bytes 1572864 | tf_op jit(solution)/shard_map/pack/pallas_call | solution.py:80
  112.3 2.1 collective-permute-start.4
  114.3 10.3 %collective-permute-start.11 = (bf16[448,256]{1,0:T(8,128)(2,1)}, bf16[448,256]{1,0:T(8,128)(2,1)S(1)}, u32[]{:S(2)}, u32[]{:S(2)}) collective-permute-start(bf16[448,256]{1,0:T(8,128)(2,1)} %get-tuple-element.47), channel_id=1, source_target_pairs={{0,14},{1,15},{2,12},{3,13},{4,10},{5,11},{6,8},{7,9},{8,6},{9,7},... | collective-permute-start | bytes 688136 | tf_op jit(solution)/shard_map/ppermute | solution.py:245
  124.6 4.3 %collective-permute-start.8 = (bf16[448,256]{1,0:T(8,128)(2,1)}, bf16[448,256]{1,0:T(8,128)(2,1)S(1)}, u32[]{:S(2)}, u32[]{:S(2)}) collective-permute-start(bf16[448,256]{1,0:T(8,128)(2,1)} %get-tuple-element.44), channel_id=1, source_target_pairs={{0,2},{1,3},{2,0},{3,1},{4,6},{5,7},{6,4},{7,5},{8,10},{9,11},{10,... | collective-permute-start | bytes 688136 | tf_op jit(solution)/shard_map/ppermute | solution.py:245
  128.9 4.7 %collective-permute-done.10.refs_3_ = bf16[448,256]{1,0:T(8,128)(2,1)S(1)} collective-permute-done((bf16[448,256]{1,0:T(8,128)(2,1)}, bf16[448,256]{1,0:T(8,128)(2,1)S(1)}, u32[]{:S(2)}, u32[]{:S(2)}) %collective-permute-start.10) | collective-permute-done | bytes 229408 | tf_op jit(solution)/shard_map/ppermute | solution.py:245
  133.6 2.3 %pack.12 = (bf16[768,256]{1,0:T(8,128)(2,1)}, bf16[768,256]{1,0:T(8,128)(2,1)}, bf16[768,256]{1,0:T(8,128)(2,1)}) custom-call(bf16[2,3,8,64,1024]{4,3,2,1,0:T(8,128)(2,1)} %refs_0_.13), custom_call_target="tpu_custom_call" | custom-call | bytes 1179648 | tf_op jit(solution)/shard_map/pack/pallas_call | solution.py:80
  135.9 17.5 %collective-permute-done.11.refs_4_ = bf16[448,256]{1,0:T(8,128)(2,1)S(1)} collective-permute-done((bf16[448,256]{1,0:T(8,128)(2,1)}, bf16[448,256]{1,0:T(8,128)(2,1)S(1)}, u32[]{:S(2)}, u32[]{:S(2)}) %collective-permute-start.11) | collective-permute-done | bytes 229408 | tf_op jit(solution)/shard_map/ppermute | solution.py:245
  153.4 4.9 %collective-permute-done.8.refs_1_ = bf16[448,256]{1,0:T(8,128)(2,1)S(1)} collective-permute-done((bf16[448,256]{1,0:T(8,128)(2,1)}, bf16[448,256]{1,0:T(8,128)(2,1)S(1)}, u32[]{:S(2)}, u32[]{:S(2)}) %collective-permute-start.8) | collective-permute-done | bytes 229408 | tf_op jit(solution)/shard_map/ppermute | solution.py:245
  158.3 5.0 %collective-permute-done.9.refs_2_ = bf16[448,256]{1,0:T(8,128)(2,1)S(1)} collective-permute-done((bf16[448,256]{1,0:T(8,128)(2,1)}, bf16[448,256]{1,0:T(8,128)(2,1)S(1)}, u32[]{:S(2)}, u32[]{:S(2)}) %collective-permute-start.9) | collective-permute-done | bytes 229408 | tf_op jit(solution)/shard_map/ppermute | solution.py:245
  163.3 0.5 collective-permute-start.13
  163.8 1.3 collective-permute-start.14
  165.1 6.6 %collective-permute-done.6.refs_3_ = bf16[768,256]{1,0:T(8,128)(2,1)S(1)} collective-permute-done((bf16[768,256]{1,0:T(8,128)(2,1)}, bf16[768,256]{1,0:T(8,128)(2,1)S(1)}, u32[]{:S(2)}, u32[]{:S(2)}) %collective-permute-start.6) | collective-permute-done | bytes 393248 | tf_op jit(solution)/shard_map/ppermute | solution.py:245
  171.8 9.7 %collective-permute-done.7.refs_4_ = bf16[768,256]{1,0:T(8,128)(2,1)S(1)} collective-permute-done((bf16[768,256]{1,0:T(8,128)(2,1)}, bf16[768,256]{1,0:T(8,128)(2,1)S(1)}, u32[]{:S(2)}, u32[]{:S(2)}) %collective-permute-start.7) | collective-permute-done | bytes 393248 | tf_op jit(solution)/shard_map/ppermute | solution.py:245
  181.4 2.2 %collective-permute-start.32 = (bf16[128,256]{1,0:T(8,128)(2,1)S(1)}, bf16[128,256]{1,0:T(8,128)(2,1)S(1)}, u32[]{:S(2)}, u32[]{:S(2)}) collective-permute-start(bf16[128,256]{1,0:T(8,128)(2,1)S(1)} %get-tuple-element.67), channel_id=1, source_target_pairs={{0,11},{1,10},{2,9},{3,8},{4,15},{5,14},{6,13},{7,12},{8,3},{9,2},... | collective-permute-start | bytes 196616 | tf_op jit(solution)/shard_map/ppermute | solution.py:245
  183.6 1.9 collective-permute-start.33
  185.5 5.7 %collective-permute-done.13.refs_2_ = bf16[768,256]{1,0:T(8,128)(2,1)S(1)} collective-permute-done((bf16[768,256]{1,0:T(8,128)(2,1)}, bf16[768,256]{1,0:T(8,128)(2,1)S(1)}, u32[]{:S(2)}, u32[]{:S(2)}) %collective-permute-start.13) | collective-permute-done | bytes 393248 | tf_op jit(solution)/shard_map/ppermute | solution.py:245
  191.3 0.0 collective-permute-start.34
  191.3 8.3 %collective-permute-done.14.refs_3_ = bf16[768,256]{1,0:T(8,128)(2,1)S(1)} collective-permute-done((bf16[768,256]{1,0:T(8,128)(2,1)}, bf16[768,256]{1,0:T(8,128)(2,1)S(1)}, u32[]{:S(2)}, u32[]{:S(2)}) %collective-permute-start.14) | collective-permute-done | bytes 393248 | tf_op jit(solution)/shard_map/ppermute | solution.py:245
  199.6 1.1 collective-permute-start.35
  200.8 1.7 pack.7.refs_0_
  202.4 0.0 copy-start.1
  202.5 1.0 copy-done.1
  203.4 0.9 unpack.8.refs_0_
  204.4 0.8 unpack.9.refs_0_
  205.2 1.1 unpack.10.refs_0_
  206.3 1.7 unpack.11.refs_0_
  208.0 1.3 unpack.12.refs_0_
  209.3 1.4 unpack.13.refs_0_
  210.7 1.2 unpack.14
  212.0 0.6 copy.11
  212.6 1.0 unpack.15
  (32 shorter events, 0.1 us)
Async XLA Ops:
  24.9 4.5 %collective-permute-start.15 = (f32[2,256]{1,0:T(2,128)S(1)}, f32[2,256]{1,0:T(2,128)S(1)}, u32[]{:S(2)}, u32[]{:S(2)}) collective-permute-start(f32[2,256]{1,0:T(2,128)S(1)} %reshape.13), channel_id=1, source_target_pairs={{0,16},{16,0},{1,17},{17,1},{2,18},{18,2},{3,19},{19,3},{4,20},{20... | collective-permute-start | bytes 6152 | tf_op jit(solution)/shard_map/ppermute | solution.py:272
  29.5 1.2 collective-permute-start.16
  30.6 2.8 %copy-start = (bf16[2,3,8,64,1024]{4,3,2,1,0:T(8,128)(2,1)S(1)}, bf16[2,3,8,64,1024]{4,3,2,1,0:T(8,128)(2,1)}, u32[]{:S(2)}) copy-start(bf16[2,3,8,64,1024]{4,3,2,1,0:T(8,128)(2,1)} %refs_0_.13) | copy-start | bytes 18874372
  33.9 17.2 %collective-permute-start.28 = (bf16[128,256]{1,0:T(8,128)(2,1)S(1)}, bf16[128,256]{1,0:T(8,128)(2,1)S(1)}, u32[]{:S(2)}, u32[]{:S(2)}) collective-permute-start(bf16[128,256]{1,0:T(8,128)(2,1)S(1)} %get-tuple-element.63), channel_id=1, source_target_pairs={{0,10},{1,11},{2,8},{3,9},{4,14},{5,15},{6,12},{7,13},{8,2},{9,3},... | collective-permute-start | bytes 196616 | tf_op jit(solution)/shard_map/ppermute | solution.py:245
  38.1 5.1 %collective-permute-start.25 = (bf16[8,256]{1,0:T(8,128)(2,1)S(1)}, bf16[8,256]{1,0:T(8,128)(2,1)S(1)}, u32[]{:S(2)}, u32[]{:S(2)}) collective-permute-start(bf16[8,256]{1,0:T(8,128)(2,1)S(1)} %get-tuple-element.59), channel_id=1, source_target_pairs={{0,1},{1,0},{2,3},{3,2},{4,5},{5,4},{6,7},{7,6},{8,9},{9,8},{10,11... | collective-permute-start | bytes 12296 | tf_op jit(solution)/shard_map/ppermute | solution.py:245
  39.7 11.8 %collective-permute-start.29 = (bf16[128,256]{1,0:T(8,128)(2,1)S(1)}, bf16[128,256]{1,0:T(8,128)(2,1)S(1)}, u32[]{:S(2)}, u32[]{:S(2)}) collective-permute-start(bf16[128,256]{1,0:T(8,128)(2,1)S(1)} %get-tuple-element.64), channel_id=1, source_target_pairs={{0,14},{1,15},{2,12},{3,13},{4,10},{5,11},{6,8},{7,9},{8,6},{9,7},... | collective-permute-start | bytes 196616 | tf_op jit(solution)/shard_map/ppermute | solution.py:245
  39.7 11.8 %collective-permute-start.30 = (bf16[128,256]{1,0:T(8,128)(2,1)S(1)}, bf16[128,256]{1,0:T(8,128)(2,1)S(1)}, u32[]{:S(2)}, u32[]{:S(2)}) collective-permute-start(bf16[128,256]{1,0:T(8,128)(2,1)S(1)} %get-tuple-element.65), channel_id=1, source_target_pairs={{0,2},{1,3},{2,0},{3,1},{4,6},{5,7},{6,4},{7,5},{8,10},{9,11},{10,... | collective-permute-start | bytes 196616 | tf_op jit(solution)/shard_map/ppermute | solution.py:245
  41.7 4.5 %collective-permute-start.26 = (bf16[8,256]{1,0:T(8,128)(2,1)S(1)}, bf16[8,256]{1,0:T(8,128)(2,1)S(1)}, u32[]{:S(2)}, u32[]{:S(2)}) collective-permute-start(bf16[8,256]{1,0:T(8,128)(2,1)S(1)} %get-tuple-element.60), channel_id=1, source_target_pairs={{0,9},{1,8},{2,11},{3,10},{4,13},{5,12},{6,15},{7,14},{8,1},{9,0},... | collective-permute-start | bytes 12296 | tf_op jit(solution)/shard_map/ppermute | solution.py:245
  43.1 3.6 %collective-permute-start.27 = (bf16[8,256]{1,0:T(8,128)(2,1)S(1)}, bf16[8,256]{1,0:T(8,128)(2,1)S(1)}, u32[]{:S(2)}, u32[]{:S(2)}) collective-permute-start(bf16[8,256]{1,0:T(8,128)(2,1)S(1)} %get-tuple-element.61), channel_id=1, source_target_pairs={{0,8},{1,9},{2,10},{3,11},{4,12},{5,13},{6,14},{7,15},{8,0},{9,1},... | collective-permute-start | bytes 12296 | tf_op jit(solution)/shard_map/ppermute | solution.py:245
  46.2 9.8 %collective-permute-start.18 = (bf16[192,256]{1,0:T(8,128)(2,1)S(1)}, bf16[192,256]{1,0:T(8,128)(2,1)S(1)}, u32[]{:S(2)}, u32[]{:S(2)}) collective-permute-start(bf16[192,256]{1,0:T(8,128)(2,1)S(1)} %get-tuple-element.52), channel_id=1, source_target_pairs={{0,7},{1,6},{2,5},{3,4},{4,3},{5,2},{6,1},{7,0},{8,15},{9,14},{10,... | collective-permute-start | bytes 294920 | tf_op jit(solution)/shard_map/ppermute | solution.py:245
  46.8 11.5 %collective-permute-start.20 = (bf16[192,256]{1,0:T(8,128)(2,1)S(1)}, bf16[192,256]{1,0:T(8,128)(2,1)S(1)}, u32[]{:S(2)}, u32[]{:S(2)}) collective-permute-start(bf16[192,256]{1,0:T(8,128)(2,1)S(1)} %get-tuple-element.54), channel_id=1, source_target_pairs={{0,15},{1,14},{2,13},{3,12},{4,11},{5,10},{6,9},{7,8},{8,7},{9,6},... | collective-permute-start | bytes 294920 | tf_op jit(solution)/shard_map/ppermute | solution.py:245
  51.2 30.0 %collective-permute-start.17 = (bf16[200,256]{1,0:T(8,128)(2,1)S(1)}, bf16[200,256]{1,0:T(8,128)(2,1)S(1)}, u32[]{:S(2)}, u32[]{:S(2)}) collective-permute-start(bf16[200,256]{1,0:T(8,128)(2,1)S(1)} %get-tuple-element.51), channel_id=1, source_target_pairs={{0,3},{1,2},{2,1},{3,0},{4,7},{5,6},{6,5},{7,4},{8,11},{9,10},{10,... | collective-permute-start | bytes 307208 | tf_op jit(solution)/shard_map/ppermute | solution.py:245
  51.4 27.7 %collective-permute-start.22 = (bf16[192,256]{1,0:T(8,128)(2,1)S(1)}, bf16[192,256]{1,0:T(8,128)(2,1)S(1)}, u32[]{:S(2)}, u32[]{:S(2)}) collective-permute-start(bf16[192,256]{1,0:T(8,128)(2,1)S(1)} %get-tuple-element.56), channel_id=1, source_target_pairs={{0,6},{1,7},{2,4},{3,5},{4,2},{5,3},{6,0},{7,1},{8,14},{9,15},{10,... | collective-permute-start | bytes 294920 | tf_op jit(solution)/shard_map/ppermute | solution.py:245
  51.4 29.7 %collective-permute-start.24 = (bf16[192,256]{1,0:T(8,128)(2,1)S(1)}, bf16[192,256]{1,0:T(8,128)(2,1)S(1)}, u32[]{:S(2)}, u32[]{:S(2)}) collective-permute-start(bf16[192,256]{1,0:T(8,128)(2,1)S(1)} %get-tuple-element.58), channel_id=1, source_target_pairs={{0,14},{1,15},{2,12},{3,13},{4,10},{5,11},{6,8},{7,9},{8,6},{9,7},... | collective-permute-start | bytes 294920 | tf_op jit(solution)/shard_map/ppermute | solution.py:245
  56.0 56.2 %collective-permute-start.1 = (bf16[448,256]{1,0:T(8,128)(2,1)}, bf16[448,256]{1,0:T(8,128)(2,1)S(1)}, u32[]{:S(2)}, u32[]{:S(2)}) collective-permute-start(bf16[448,256]{1,0:T(8,128)(2,1)} %get-tuple-element.37), channel_id=1, source_target_pairs={{0,7},{1,6},{2,5},{3,4},{4,3},{5,2},{6,1},{7,0},{8,15},{9,14},{10,... | collective-permute-start | bytes 688136 | tf_op jit(solution)/shard_map/ppermute | solution.py:245
  58.3 56.0 %collective-permute-start.2 = (bf16[448,256]{1,0:T(8,128)(2,1)}, bf16[448,256]{1,0:T(8,128)(2,1)S(1)}, u32[]{:S(2)}, u32[]{:S(2)}) collective-permute-start(bf16[448,256]{1,0:T(8,128)(2,1)} %get-tuple-element.38), channel_id=1, source_target_pairs={{0,11},{1,10},{2,9},{3,8},{4,15},{5,14},{6,13},{7,12},{8,3},{9,2},... | collective-permute-start | bytes 688136 | tf_op jit(solution)/shard_map/ppermute | solution.py:245
  79.1 8.5 %collective-permute-start.19 = (bf16[200,256]{1,0:T(8,128)(2,1)S(1)}, bf16[200,256]{1,0:T(8,128)(2,1)S(1)}, u32[]{:S(2)}, u32[]{:S(2)}) collective-permute-start(bf16[200,256]{1,0:T(8,128)(2,1)S(1)} %get-tuple-element.53), channel_id=1, source_target_pairs={{0,11},{1,10},{2,9},{3,8},{4,15},{5,14},{6,13},{7,12},{8,3},{9,2},... | collective-permute-start | bytes 307208 | tf_op jit(solution)/shard_map/ppermute | solution.py:245
  81.2 25.6 %collective-permute-start.21 = (bf16[200,256]{1,0:T(8,128)(2,1)S(1)}, bf16[200,256]{1,0:T(8,128)(2,1)S(1)}, u32[]{:S(2)}, u32[]{:S(2)}) collective-permute-start(bf16[200,256]{1,0:T(8,128)(2,1)S(1)} %get-tuple-element.55), channel_id=1, source_target_pairs={{0,2},{1,3},{2,0},{3,1},{4,6},{5,7},{6,4},{7,5},{8,10},{9,11},{10,... | collective-permute-start | bytes 307208 | tf_op jit(solution)/shard_map/ppermute | solution.py:245
  81.2 27.7 %collective-permute-start.23 = (bf16[200,256]{1,0:T(8,128)(2,1)S(1)}, bf16[200,256]{1,0:T(8,128)(2,1)S(1)}, u32[]{:S(2)}, u32[]{:S(2)}) collective-permute-start(bf16[200,256]{1,0:T(8,128)(2,1)S(1)} %get-tuple-element.57), channel_id=1, source_target_pairs={{0,10},{1,11},{2,8},{3,9},{4,14},{5,15},{6,12},{7,13},{8,2},{9,3},... | collective-permute-start | bytes 307208 | tf_op jit(solution)/shard_map/ppermute | solution.py:245
  87.6 26.7 %collective-permute-start.3 = (bf16[448,256]{1,0:T(8,128)(2,1)}, bf16[448,256]{1,0:T(8,128)(2,1)S(1)}, u32[]{:S(2)}, u32[]{:S(2)}) collective-permute-start(bf16[448,256]{1,0:T(8,128)(2,1)} %get-tuple-element.39), channel_id=1, source_target_pairs={{0,15},{1,14},{2,13},{3,12},{4,11},{5,10},{6,9},{7,8},{8,7},{9,6},... | collective-permute-start | bytes 688136 | tf_op jit(solution)/shard_map/ppermute | solution.py:245
  106.8 17.8 %collective-permute-start = (bf16[448,256]{1,0:T(8,128)(2,1)}, bf16[448,256]{1,0:T(8,128)(2,1)S(1)}, u32[]{:S(2)}, u32[]{:S(2)}) collective-permute-start(bf16[448,256]{1,0:T(8,128)(2,1)} %pack.8), channel_id=1, source_target_pairs={{0,3},{1,2},{2,1},{3,0},{4,7},{5,6},{6,5},{7,4},{8,11},{9,10},{10,... | collective-permute-start | bytes 688136 | tf_op jit(solution)/shard_map/ppermute | solution.py:245
  108.9 24.7 %collective-permute-start.10 = (bf16[448,256]{1,0:T(8,128)(2,1)}, bf16[448,256]{1,0:T(8,128)(2,1)S(1)}, u32[]{:S(2)}, u32[]{:S(2)}) collective-permute-start(bf16[448,256]{1,0:T(8,128)(2,1)} %get-tuple-element.46), channel_id=1, source_target_pairs={{0,10},{1,11},{2,8},{3,9},{4,14},{5,15},{6,12},{7,13},{8,2},{9,3},... | collective-permute-start | bytes 688136 | tf_op jit(solution)/shard_map/ppermute | solution.py:245
  112.3 51.0 %collective-permute-start.4 = (bf16[768,256]{1,0:T(8,128)(2,1)}, bf16[768,256]{1,0:T(8,128)(2,1)S(1)}, u32[]{:S(2)}, u32[]{:S(2)}) collective-permute-start(bf16[768,256]{1,0:T(8,128)(2,1)} %get-tuple-element.40), channel_id=1, source_target_pairs={{0,1},{1,0},{2,3},{3,2},{4,5},{5,4},{6,7},{7,6},{8,9},{9,8},{10,11... | collective-permute-start | bytes 1179656 | tf_op jit(solution)/shard_map/ppermute | solution.py:245
  114.3 49.5 %collective-permute-start.5 = (bf16[768,256]{1,0:T(8,128)(2,1)}, bf16[768,256]{1,0:T(8,128)(2,1)S(1)}, u32[]{:S(2)}, u32[]{:S(2)}) collective-permute-start(bf16[768,256]{1,0:T(8,128)(2,1)} %get-tuple-element.41), channel_id=1, source_target_pairs={{0,5},{1,4},{2,7},{3,6},{4,1},{5,0},{6,3},{7,2},{8,13},{9,12},{10,... | collective-permute-start | bytes 1179656 | tf_op jit(solution)/shard_map/ppermute | solution.py:245
  114.3 39.0 %collective-permute-start.11 = (bf16[448,256]{1,0:T(8,128)(2,1)}, bf16[448,256]{1,0:T(8,128)(2,1)S(1)}, u32[]{:S(2)}, u32[]{:S(2)}) collective-permute-start(bf16[448,256]{1,0:T(8,128)(2,1)} %get-tuple-element.47), channel_id=1, source_target_pairs={{0,14},{1,15},{2,12},{3,13},{4,10},{5,11},{6,8},{7,9},{8,6},{9,7},... | collective-permute-start | bytes 688136 | tf_op jit(solution)/shard_map/ppermute | solution.py:245
  124.6 33.6 %collective-permute-start.8 = (bf16[448,256]{1,0:T(8,128)(2,1)}, bf16[448,256]{1,0:T(8,128)(2,1)S(1)}, u32[]{:S(2)}, u32[]{:S(2)}) collective-permute-start(bf16[448,256]{1,0:T(8,128)(2,1)} %get-tuple-element.44), channel_id=1, source_target_pairs={{0,2},{1,3},{2,0},{3,1},{4,6},{5,7},{6,4},{7,5},{8,10},{9,11},{10,... | collective-permute-start | bytes 688136 | tf_op jit(solution)/shard_map/ppermute | solution.py:245
  133.6 29.7 %collective-permute-start.9 = (bf16[448,256]{1,0:T(8,128)(2,1)}, bf16[448,256]{1,0:T(8,128)(2,1)S(1)}, u32[]{:S(2)}, u32[]{:S(2)}) collective-permute-start(bf16[448,256]{1,0:T(8,128)(2,1)} %get-tuple-element.45), channel_id=1, source_target_pairs={{0,6},{1,7},{2,4},{3,5},{4,2},{5,3},{6,0},{7,1},{8,14},{9,15},{10,... | collective-permute-start | bytes 688136 | tf_op jit(solution)/shard_map/ppermute | solution.py:245
  153.4 18.4 %collective-permute-start.6 = (bf16[768,256]{1,0:T(8,128)(2,1)}, bf16[768,256]{1,0:T(8,128)(2,1)S(1)}, u32[]{:S(2)}, u32[]{:S(2)}) collective-permute-start(bf16[768,256]{1,0:T(8,128)(2,1)} %get-tuple-element.42), channel_id=1, source_target_pairs={{0,9},{1,8},{2,11},{3,10},{4,13},{5,12},{6,15},{7,14},{8,1},{9,0},... | collective-permute-start | bytes 1179656 | tf_op jit(solution)/shard_map/ppermute | solution.py:245
  158.3 23.2 %collective-permute-start.7 = (bf16[768,256]{1,0:T(8,128)(2,1)}, bf16[768,256]{1,0:T(8,128)(2,1)S(1)}, u32[]{:S(2)}, u32[]{:S(2)}) collective-permute-start(bf16[768,256]{1,0:T(8,128)(2,1)} %get-tuple-element.43), channel_id=1, source_target_pairs={{0,13},{1,12},{2,15},{3,14},{4,9},{5,8},{6,11},{7,10},{8,5},{9,4},... | collective-permute-start | bytes 1179656 | tf_op jit(solution)/shard_map/ppermute | solution.py:245
  163.3 20.3 %collective-permute-start.12 = (bf16[768,256]{1,0:T(8,128)(2,1)}, bf16[768,256]{1,0:T(8,128)(2,1)S(1)}, u32[]{:S(2)}, u32[]{:S(2)}) collective-permute-start(bf16[768,256]{1,0:T(8,128)(2,1)} %get-tuple-element.48), channel_id=1, source_target_pairs={{0,4},{1,5},{2,6},{3,7},{4,0},{5,1},{6,2},{7,3},{8,12},{9,13},{10,... | collective-permute-start | bytes 1179656 | tf_op jit(solution)/shard_map/ppermute | solution.py:245
  163.3 28.0 %collective-permute-start.13 = (bf16[768,256]{1,0:T(8,128)(2,1)}, bf16[768,256]{1,0:T(8,128)(2,1)S(1)}, u32[]{:S(2)}, u32[]{:S(2)}) collective-permute-start(bf16[768,256]{1,0:T(8,128)(2,1)} %get-tuple-element.49), channel_id=1, source_target_pairs={{0,8},{1,9},{2,10},{3,11},{4,12},{5,13},{6,14},{7,15},{8,0},{9,1},... | collective-permute-start | bytes 1179656 | tf_op jit(solution)/shard_map/ppermute | solution.py:245
  163.8 35.8 %collective-permute-start.14 = (bf16[768,256]{1,0:T(8,128)(2,1)}, bf16[768,256]{1,0:T(8,128)(2,1)S(1)}, u32[]{:S(2)}, u32[]{:S(2)}) collective-permute-start(bf16[768,256]{1,0:T(8,128)(2,1)} %get-tuple-element.50), channel_id=1, source_target_pairs={{0,12},{1,13},{2,14},{3,15},{4,8},{5,9},{6,10},{7,11},{8,4},{9,5},... | collective-permute-start | bytes 1179656 | tf_op jit(solution)/shard_map/ppermute | solution.py:245
  171.8 40.8 %collective-permute-start.31 = (bf16[128,256]{1,0:T(8,128)(2,1)S(1)}, bf16[128,256]{1,0:T(8,128)(2,1)S(1)}, u32[]{:S(2)}, u32[]{:S(2)}) collective-permute-start(bf16[128,256]{1,0:T(8,128)(2,1)S(1)} %get-tuple-element.66), channel_id=1, source_target_pairs={{0,6},{1,7},{2,4},{3,5},{4,2},{5,3},{6,0},{7,1},{8,14},{9,15},{10,... | collective-permute-start | bytes 196616 | tf_op jit(solution)/shard_map/ppermute | solution.py:245
  181.4 31.2 %collective-permute-start.32 = (bf16[128,256]{1,0:T(8,128)(2,1)S(1)}, bf16[128,256]{1,0:T(8,128)(2,1)S(1)}, u32[]{:S(2)}, u32[]{:S(2)}) collective-permute-start(bf16[128,256]{1,0:T(8,128)(2,1)S(1)} %get-tuple-element.67), channel_id=1, source_target_pairs={{0,11},{1,10},{2,9},{3,8},{4,15},{5,14},{6,13},{7,12},{8,3},{9,2},... | collective-permute-start | bytes 196616 | tf_op jit(solution)/shard_map/ppermute | solution.py:245
  183.6 29.0 %collective-permute-start.33 = (bf16[128,256]{1,0:T(8,128)(2,1)S(1)}, bf16[128,256]{1,0:T(8,128)(2,1)S(1)}, u32[]{:S(2)}, u32[]{:S(2)}) collective-permute-start(bf16[128,256]{1,0:T(8,128)(2,1)S(1)} %get-tuple-element.68), channel_id=1, source_target_pairs={{0,15},{1,14},{2,13},{3,12},{4,11},{5,10},{6,9},{7,8},{8,7},{9,6},... | collective-permute-start | bytes 196616 | tf_op jit(solution)/shard_map/ppermute | solution.py:245
  191.3 21.3 %collective-permute-start.34 = (bf16[128,256]{1,0:T(8,128)(2,1)S(1)}, bf16[128,256]{1,0:T(8,128)(2,1)S(1)}, u32[]{:S(2)}, u32[]{:S(2)}) collective-permute-start(bf16[128,256]{1,0:T(8,128)(2,1)S(1)} %get-tuple-element.69), channel_id=1, source_target_pairs={{0,3},{1,2},{2,1},{3,0},{4,7},{5,6},{6,5},{7,4},{8,11},{9,10},{10,... | collective-permute-start | bytes 196616 | tf_op jit(solution)/shard_map/ppermute | solution.py:245
  199.6 13.0 %collective-permute-start.35 = (bf16[128,256]{1,0:T(8,128)(2,1)S(1)}, bf16[128,256]{1,0:T(8,128)(2,1)S(1)}, u32[]{:S(2)}, u32[]{:S(2)}) collective-permute-start(bf16[128,256]{1,0:T(8,128)(2,1)S(1)} %get-tuple-element.70), channel_id=1, source_target_pairs={{0,7},{1,6},{2,5},{3,4},{4,3},{5,2},{6,1},{7,0},{8,15},{9,14},{10,... | collective-permute-start | bytes 196616 | tf_op jit(solution)/shard_map/ppermute | solution.py:245
  202.4 1.0 copy-start.1

commit v2 on v0

--- a/solution.py
+++ b/solution.py
@@ -25,6 +25,20 @@
     if is_power(n):
         return i ^ step
     return (i - step + n) % n if back else (i + step) % n
+
+
+def add_groups(totals, slab_n, py_n):
+    if not (is_power(slab_n) and is_power(py_n)):
+        return lax.psum(totals, ("slab", "py"))
+    bits = lambda n: [1 << k for k in range(n.bit_length() - 1)]
+    swaps = [(min(1, slab_n - 1), p) for p in bits(py_n)[1:]]
+    swaps += [(s, 0) for s in bits(slab_n)] + [(0, p) for p in bits(py_n)[:1]]
+    for s, p in swaps:
+        pairs = [
+            (i * py_n + j, (i ^ s) * py_n + (j ^ p)) for i in range(slab_n) for j in range(py_n)
+        ]
+        totals = totals + lax.ppermute(totals, ("slab", "py"), pairs)
+    return totals
 
 
 def split3(x):
@@ -116,12 +130,12 @@
             ).start()
         if more:
             extra = pieces[k][pl.ds(size, 8), :].astype(jnp.float32)
-            each[from_y * px_n + from_x] = (extra[0:2] + extra[2:4]) + extra[4:6]
+            each[from_x] = (extra[0:2] + extra[2:4]) + extra[4:6]
     if scale is not None:
         a, b, c = [x.astype(jnp.float32) for x in split3(mine[...])]
-        each[me_y * px_n + me_x] = (a + b) + c
+        each[me_x] = (a + b) + c
         total = each[0]
-        for i in range(1, py_n * px_n):
+        for i in range(1, px_n):
             total = total + each[i]
         spectrum[...] = total * scale
     for k, (_, _, first, last, _) in enumerate(steps):
@@ -142,7 +156,7 @@
     if scale is not None:
         outs.append(jax.ShapeDtypeStruct(mine.shape, jnp.float32))
         out_specs.append(vmem)
-        extra = [pltpu.VMEM((py_n * px_n,) + mine.shape, jnp.float32)]
+        extra = [pltpu.VMEM((px_n,) + mine.shape, jnp.float32)]
     done = pl.pallas_call(
         functools.partial(unpack_kernel, steps, sizes, planes, base is not None, scale),
         out_shape=outs,
@@ -257,14 +271,10 @@
     own = pack(state, None, [(0, 0, 0, blocks, False)], sizes, planes)
     totals = bin_energy(state, shells)
     totals = totals.reshape(SHELLS // LANES, LANES)
-    shift = 1 if is_power(slab_n) else slab_n
-    if not is_power(slab_n):
-        totals = lax.psum(totals, "slab")
-    while shift < slab_n:
-        totals = totals + lax.ppermute(totals, "slab", [(i, partner(i, shift, slab_n)) for i in range(slab_n)])
-        shift *= 2
-    mid = part(far, cut1, cut2, True) + part(near, blocks, blocks, True)
-    late = part(far, cut2, blocks)
+    totals = add_groups(totals, slab_n, py_n)
+    mid = [s + (cut1, cut2, s[0] == 0) for s in far]
+    mid += part([s for s in near if s[0] == 0], blocks, blocks, True)
+    late = part([(a, b) for b in range(px_n // 2, px_n) for a in [*range(py_n // 2, py_n), *range(py_n // 2)]], cut2, blocks)
     packed = pack(state, totals, mid + late, sizes, planes)
     got = [send(x, s) for x, s in zip(packed, mid + late)]
     modes = slab_n * py_n * px_n * planes_all * rows * columns
@@ -275,7 +285,10 @@
     out, spectrum = unpack(
         out, totals, got[: len(mid)], mid, sizes, planes, rows, scale=0.5 * SHELLS / modes
     )
-    out = unpack(out, None, got[len(mid) :], late, sizes, planes, rows)
+    got, start = got[len(mid) :], 0
+    for stop in (len(late) // 2, len(late) * 3 // 4, len(late)):
+        out = unpack(out, None, got[start:stop], late[start:stop], sizes, planes, rows)
+        start = stop
     restored = out.reshape(2, 3, planes, py_n * px_n * rows, columns // px_n)
     return (restored, spectrum.reshape(SHELLS))
 

time: 216 us -> 216 us (level); the launches traced: 212 us -> 216 us
  waiting for transfers between devices: 54.6 us -> 104 us
  starting transfers between devices: 106 us -> 58.7 us
    ppermute x38 -> x32, starting transfers between devices: 103 us -> 52.8 us  [send(): return lax.ppermute(x, ('py', 'px'), pairs)]
    ppermute x38 -> x32, waiting for transfers between devices: 53 us -> 99.7 us  [send(): return lax.ppermute(x, ('py', 'px'), pairs)]
    ppermute x1 -> x3, starting transfers between devices: 2.97 us -> 5.9 us  [add_groups(): totals = totals + lax.ppermute(totals, ('slab', 'py'), pairs)]
    ppermute x1 -> x3, waiting for transfers between devices: 1.56 us -> 4.34 us  [add_groups(): totals = totals + lax.ppermute(totals, ('slab', 'py'), pairs)]
    pallas_call x8 -> x10, Pallas kernels: 9.57 us -> 10.7 us  [unpack(): pl.pallas_call(functools.partial(unpack_kernel, steps, sizes, planes, bas...]
  transfers between devices with their start and end apart: 39 -> 35, of which waited for: 11 -> 14; matrix products, arithmetic and copies ran while one was open for 0% -> 0% of each run, Pallas kernels for 10% -> 10%
where the time goes in v2:
time: 216 us
  waiting for transfers between devices  104 us (48%)
  starting transfers between devices  58.7 us (27%)
  Pallas kernels  46.8 us (22%)
  local copies, waits for them, and re-layouts  5.13 us (2%)
    ppermute x32, waiting for transfers between devices, send(): return lax.ppermute(x, ('py', 'px'), pairs)  99.7 us
    ppermute x32, starting transfers between devices, send(): return lax.ppermute(x, ('py', 'px'), pairs)  52.8 us
    pallas_call x1, Pallas kernels, bin_energy(): pl.pallas_call(bin_kernel, grid=(planes,), out_shape=jax.ShapeDtypeStruct...  23.5 us
    pallas_call x7, Pallas kernels, pack(): pl.pallas_call(functools.partial(pack_kernel, steps, sizes, planes, total...  12.5 us
    pallas_call x10, Pallas kernels, unpack(): pl.pallas_call(functools.partial(unpack_kernel, steps, sizes, planes, bas...  10.7 us
    ppermute x3, starting transfers between devices, add_groups(): totals = totals + lax.ppermute(totals, ('slab', 'py'), pairs)  5.9 us
    unnamed x5, local copies, waits for them, and re-layouts  4.36 us
    ppermute x3, waiting for transfers between devices, add_groups(): totals = totals + lax.ppermute(totals, ('slab', 'py'), pairs)  4.34 us
  transfers between devices with their start and end apart: 35, of which 14 were waited for; matrix products, arithmetic and copies ran while one was open for 0% of the time, Pallas kernels for 10%

profile of v2, /device:TPU:0, one launch (start us, length us, event | category | flops | bytes accessed | tf_op | source)
XLA Modules:
  0.0 215.5 jit_solution(17708402905341211186)
XLA Ops:
  0.6 23.5 %bins.1 = f32[16,32]{1,0:T(8,128)} custom-call(bf16[2,3,8,64,1024]{4,3,2,1,0:T(8,128)(2,1)} %refs_0_.13, s32[8,64,1024]{2,1,0:T(8,128)} %shells.1), custom_call_target="tpu_custom_call" | custom-call | flops 1073741824 | bytes 8388608 | tf_op jit(solution)/shard_map/bins/pallas_call | solution.py:221
  24.2 0.8 reshape.13
  24.9 3.9 %collective-permute-start.15 = (f32[2,256]{1,0:T(2,128)S(1)}, f32[2,256]{1,0:T(2,128)S(1)}, u32[]{:S(2)}, u32[]{:S(2)}) collective-permute-start(f32[2,256]{1,0:T(2,128)S(1)} %reshape.13), channel_id=1, source_target_pairs={{0,24},{4,28},{8,16},{12,20},{16,8},{20,12},{24,0},{28,4},{1,25},{... | collective-permute-start | bytes 6152 | tf_op jit(solution)/shard_map/ppermute | solution.py:40
  28.9 1.6 collective-permute-done.15
  30.4 2.0 collective-permute-start.16
  32.4 1.6 collective-permute-done.16
  34.0 0.0 collective-permute-start.17
  34.0 1.2 collective-permute-done.17
  35.2 2.8 %copy-done = bf16[2,3,8,64,1024]{4,3,2,1,0:T(8,128)(2,1)S(1)} copy-done((bf16[2,3,8,64,1024]{4,3,2,1,0:T(8,128)(2,1)S(1)}, bf16[2,3,8,64,1024]{4,3,2,1,0:T(8,128)(2,1)}, u32[]{:S(2)}) %copy-start) | copy-done | bytes 6291480
  38.0 0.5 pack.13
  38.5 4.1 %collective-permute-start.27 = (bf16[128,256]{1,0:T(8,128)(2,1)S(1)}, bf16[128,256]{1,0:T(8,128)(2,1)S(1)}, u32[]{:S(2)}, u32[]{:S(2)}) collective-permute-start(bf16[128,256]{1,0:T(8,128)(2,1)S(1)} %get-tuple-element.59), channel_id=1, source_target_pairs={{0,10},{1,11},{2,8},{3,9},{4,14},{5,15},{6,12},{7,13},{8,2},{9,3},... | collective-permute-start | bytes 196616 | tf_op jit(solution)/shard_map/ppermute | solution.py:254
  42.5 0.0 collective-permute-start.28
  42.5 1.6 collective-permute-start.26
  44.1 2.4 %collective-permute-start.29 = (bf16[128,256]{1,0:T(8,128)(2,1)S(1)}, bf16[128,256]{1,0:T(8,128)(2,1)S(1)}, u32[]{:S(2)}, u32[]{:S(2)}) collective-permute-start(bf16[128,256]{1,0:T(8,128)(2,1)S(1)} %get-tuple-element.61), channel_id=1, source_target_pairs={{0,2},{1,3},{2,0},{3,1},{4,6},{5,7},{6,4},{7,5},{8,10},{9,11},{10,... | collective-permute-start | bytes 196616 | tf_op jit(solution)/shard_map/ppermute | solution.py:254
  46.5 4.5 %collective-permute-start.20 = (bf16[192,256]{1,0:T(8,128)(2,1)S(1)}, bf16[192,256]{1,0:T(8,128)(2,1)S(1)}, u32[]{:S(2)}, u32[]{:S(2)}) collective-permute-start(bf16[192,256]{1,0:T(8,128)(2,1)S(1)} %get-tuple-element.51), channel_id=1, source_target_pairs={{0,11},{1,10},{2,9},{3,8},{4,15},{5,14},{6,13},{7,12},{8,3},{9,2},... | collective-permute-start | bytes 294920 | tf_op jit(solution)/shard_map/ppermute | solution.py:254
  51.0 0.9 collective-permute-start.21
  51.9 0.3 collective-permute-start.23
  52.2 6.4 %collective-permute-done.29.refs_3_ = bf16[128,256]{1,0:T(8,128)(2,1)S(1)} collective-permute-done((bf16[128,256]{1,0:T(8,128)(2,1)S(1)}, bf16[128,256]{1,0:T(8,128)(2,1)S(1)}, u32[]{:S(2)}, u32[]{:S(2)}) %collective-permute-start.29) | collective-permute-done | bytes 65568 | tf_op jit(solution)/shard_map/ppermute | solution.py:254
  58.6 0.2 collective-permute-start.24
  58.8 1.9 pack.9
  60.8 6.9 %collective-permute-start.1 = (bf16[448,256]{1,0:T(8,128)(2,1)}, bf16[448,256]{1,0:T(8,128)(2,1)S(1)}, u32[]{:S(2)}, u32[]{:S(2)}) collective-permute-start(bf16[448,256]{1,0:T(8,128)(2,1)} %get-tuple-element.35), channel_id=1, source_target_pairs={{0,7},{1,6},{2,5},{3,4},{4,3},{5,2},{6,1},{7,0},{8,15},{9,14},{10,... | collective-permute-start | bytes 688136 | tf_op jit(solution)/shard_map/ppermute | solution.py:254
  67.7 1.0 collective-permute-start.2
  68.7 2.9 %collective-permute-start.18 = (bf16[200,256]{1,0:T(8,128)(2,1)S(1)}, bf16[200,256]{1,0:T(8,128)(2,1)S(1)}, u32[]{:S(2)}, u32[]{:S(2)}) collective-permute-start(bf16[200,256]{1,0:T(8,128)(2,1)S(1)} %get-tuple-element.49), channel_id=1, source_target_pairs={{0,3},{1,2},{2,1},{3,0},{4,7},{5,6},{6,5},{7,4},{8,11},{9,10},{10,... | collective-permute-start | bytes 307208 | tf_op jit(solution)/shard_map/ppermute | solution.py:254
  71.6 11.4 %collective-permute-done.23.refs_7_ = bf16[192,256]{1,0:T(8,128)(2,1)S(1)} collective-permute-done((bf16[192,256]{1,0:T(8,128)(2,1)S(1)}, bf16[192,256]{1,0:T(8,128)(2,1)S(1)}, u32[]{:S(2)}, u32[]{:S(2)}) %collective-permute-start.23) | collective-permute-done | bytes 98336 | tf_op jit(solution)/shard_map/ppermute | solution.py:254
  83.0 0.8 collective-permute-start.22
  83.8 2.3 %collective-permute-done.24.refs_8_ = bf16[192,256]{1,0:T(8,128)(2,1)S(1)} collective-permute-done((bf16[192,256]{1,0:T(8,128)(2,1)S(1)}, bf16[192,256]{1,0:T(8,128)(2,1)S(1)}, u32[]{:S(2)}, u32[]{:S(2)}) %collective-permute-start.24) | collective-permute-done | bytes 98336 | tf_op jit(solution)/shard_map/ppermute | solution.py:254
  86.1 0.1 collective-permute-start.25
  86.2 1.5 pack.8
  87.8 18.8 %collective-permute-done.25.refs_9_ = bf16[192,256]{1,0:T(8,128)(2,1)S(1)} collective-permute-done((bf16[192,256]{1,0:T(8,128)(2,1)S(1)}, bf16[192,256]{1,0:T(8,128)(2,1)S(1)}, u32[]{:S(2)}, u32[]{:S(2)}) %collective-permute-start.25) | collective-permute-done | bytes 98336 | tf_op jit(solution)/shard_map/ppermute | solution.py:254
  106.6 3.2 %collective-permute-start.3 = (bf16[448,256]{1,0:T(8,128)(2,1)}, bf16[448,256]{1,0:T(8,128)(2,1)S(1)}, u32[]{:S(2)}, u32[]{:S(2)}) collective-permute-start(bf16[448,256]{1,0:T(8,128)(2,1)} %get-tuple-element.37), channel_id=1, source_target_pairs={{0,15},{1,14},{2,13},{3,12},{4,11},{5,10},{6,9},{7,8},{8,7},{9,6},... | collective-permute-start | bytes 688136 | tf_op jit(solution)/shard_map/ppermute | solution.py:254
  109.8 2.1 pack.11
  111.9 0.4 collective-permute-start
  112.3 2.5 %pack.10 = (bf16[768,256]{1,0:T(8,128)(2,1)}, bf16[768,256]{1,0:T(8,128)(2,1)}, bf16[768,256]{1,0:T(8,128)(2,1)}, bf16[768,256]{1,0:T(8,128)(2,1)}) custom-call(bf16[2,3,8,64,1024]{4,3,2,1,0:T(8,128)(2,1)} %refs_0_.13), custom_call_target="tpu_custom_call" | custom-call | bytes 1572864 | tf_op jit(solution)/shard_map/pack/pallas_call | solution.py:90
  114.9 4.0 %collective-permute-start.4 = (bf16[768,256]{1,0:T(8,128)(2,1)}, bf16[768,256]{1,0:T(8,128)(2,1)S(1)}, u32[]{:S(2)}, u32[]{:S(2)}) collective-permute-start(bf16[768,256]{1,0:T(8,128)(2,1)} %get-tuple-element.38), channel_id=1, source_target_pairs={{0,1},{1,0},{2,3},{3,2},{4,5},{5,4},{6,7},{7,6},{8,9},{9,8},{10,11... | collective-permute-start | bytes 1179656 | tf_op jit(solution)/shard_map/ppermute | solution.py:254
  118.9 11.0 %collective-permute-start.11 = (bf16[448,256]{1,0:T(8,128)(2,1)}, bf16[448,256]{1,0:T(8,128)(2,1)S(1)}, u32[]{:S(2)}, u32[]{:S(2)}) collective-permute-start(bf16[448,256]{1,0:T(8,128)(2,1)} %get-tuple-element.45), channel_id=1, source_target_pairs={{0,14},{1,15},{2,12},{3,13},{4,10},{5,11},{6,8},{7,9},{8,6},{9,7},... | collective-permute-start | bytes 688136 | tf_op jit(solution)/shard_map/ppermute | solution.py:254
  129.9 4.3 %collective-permute-start.8 = (bf16[448,256]{1,0:T(8,128)(2,1)}, bf16[448,256]{1,0:T(8,128)(2,1)S(1)}, u32[]{:S(2)}, u32[]{:S(2)}) collective-permute-start(bf16[448,256]{1,0:T(8,128)(2,1)} %get-tuple-element.42), channel_id=1, source_target_pairs={{0,2},{1,3},{2,0},{3,1},{4,6},{5,7},{6,4},{7,5},{8,10},{9,11},{10,... | collective-permute-start | bytes 688136 | tf_op jit(solution)/shard_map/ppermute | solution.py:254
  134.2 5.5 %collective-permute-done.10.refs_3_ = bf16[448,256]{1,0:T(8,128)(2,1)S(1)} collective-permute-done((bf16[448,256]{1,0:T(8,128)(2,1)}, bf16[448,256]{1,0:T(8,128)(2,1)S(1)}, u32[]{:S(2)}, u32[]{:S(2)}) %collective-permute-start.10) | collective-permute-done | bytes 229408 | tf_op jit(solution)/shard_map/ppermute | solution.py:254
  139.8 2.3 %pack.12 = (bf16[768,256]{1,0:T(8,128)(2,1)}, bf16[768,256]{1,0:T(8,128)(2,1)}, bf16[768,256]{1,0:T(8,128)(2,1)}) custom-call(bf16[2,3,8,64,1024]{4,3,2,1,0:T(8,128)(2,1)} %refs_0_.13), custom_call_target="tpu_custom_call" | custom-call | bytes 1179648 | tf_op jit(solution)/shard_map/pack/pallas_call | solution.py:90
  142.1 5.8 %collective-permute-done.11.refs_4_ = bf16[448,256]{1,0:T(8,128)(2,1)S(1)} collective-permute-done((bf16[448,256]{1,0:T(8,128)(2,1)}, bf16[448,256]{1,0:T(8,128)(2,1)S(1)}, u32[]{:S(2)}, u32[]{:S(2)}) %collective-permute-start.11) | collective-permute-done | bytes 229408 | tf_op jit(solution)/shard_map/ppermute | solution.py:254
  147.8 1.7 collective-permute-start.6
  149.5 13.9 %collective-permute-done.8.refs_1_ = bf16[448,256]{1,0:T(8,128)(2,1)S(1)} collective-permute-done((bf16[448,256]{1,0:T(8,128)(2,1)}, bf16[448,256]{1,0:T(8,128)(2,1)S(1)}, u32[]{:S(2)}, u32[]{:S(2)}) %collective-permute-start.8) | collective-permute-done | bytes 229408 | tf_op jit(solution)/shard_map/ppermute | solution.py:254
  163.4 4.5 %collective-permute-done.9.refs_2_ = bf16[448,256]{1,0:T(8,128)(2,1)S(1)} collective-permute-done((bf16[448,256]{1,0:T(8,128)(2,1)}, bf16[448,256]{1,0:T(8,128)(2,1)S(1)}, u32[]{:S(2)}, u32[]{:S(2)}) %collective-permute-start.9) | collective-permute-done | bytes 229408 | tf_op jit(solution)/shard_map/ppermute | solution.py:254
  168.0 0.1 collective-permute-start.12
  168.0 1.7 collective-permute-start.13
  169.7 0.1 collective-permute-start.14
  169.9 13.4 %collective-permute-done.7.refs_4_ = bf16[768,256]{1,0:T(8,128)(2,1)S(1)} collective-permute-done((bf16[768,256]{1,0:T(8,128)(2,1)}, bf16[768,256]{1,0:T(8,128)(2,1)S(1)}, u32[]{:S(2)}, u32[]{:S(2)}) %collective-permute-start.7) | collective-permute-done | bytes 393248 | tf_op jit(solution)/shard_map/ppermute | solution.py:254
  183.3 9.7 %collective-permute-done.13.refs_2_ = bf16[768,256]{1,0:T(8,128)(2,1)S(1)} collective-permute-done((bf16[768,256]{1,0:T(8,128)(2,1)}, bf16[768,256]{1,0:T(8,128)(2,1)S(1)}, u32[]{:S(2)}, u32[]{:S(2)}) %collective-permute-start.13) | collective-permute-done | bytes 393248 | tf_op jit(solution)/shard_map/ppermute | solution.py:254
  192.9 0.5 collective-permute-start.33
  193.4 7.9 %collective-permute-done.14.refs_3_ = bf16[768,256]{1,0:T(8,128)(2,1)S(1)} collective-permute-done((bf16[768,256]{1,0:T(8,128)(2,1)}, bf16[768,256]{1,0:T(8,128)(2,1)S(1)}, u32[]{:S(2)}, u32[]{:S(2)}) %collective-permute-start.14) | collective-permute-done | bytes 393248 | tf_op jit(solution)/shard_map/ppermute | solution.py:254
  201.3 0.1 collective-permute-start.34
  201.4 1.7 pack.7.refs_0_
  203.1 0.0 copy-start.1
  203.1 1.0 copy-done.1
  204.1 0.9 unpack.10.refs_0_
  205.0 0.8 unpack.11.refs_0_
  205.8 1.1 unpack.12.refs_0_
  206.9 1.7 unpack.13.refs_0_
  208.6 1.3 unpack.14.refs_0_
  209.9 1.4 unpack.15.refs_0_
  211.4 1.2 unpack.16
  212.6 0.6 copy.13
  213.2 0.8 unpack.17.refs_0_
  214.0 0.7 unpack.18.refs_0_
  214.8 0.7 unpack.19
  (33 shorter events, 0.1 us)
Async XLA Ops:
  24.9 5.5 %collective-permute-start.15 = (f32[2,256]{1,0:T(2,128)S(1)}, f32[2,256]{1,0:T(2,128)S(1)}, u32[]{:S(2)}, u32[]{:S(2)}) collective-permute-start(f32[2,256]{1,0:T(2,128)S(1)} %reshape.13), channel_id=1, source_target_pairs={{0,24},{4,28},{8,16},{12,20},{16,8},{20,12},{24,0},{28,4},{1,25},{... | collective-permute-start | bytes 6152 | tf_op jit(solution)/shard_map/ppermute | solution.py:40
  30.4 3.6 %collective-permute-start.16 = (f32[2,256]{1,0:T(2,128)S(1)}, f32[2,256]{1,0:T(2,128)S(1)}, u32[]{:S(2)}, u32[]{:S(2)}) collective-permute-start(f32[2,256]{1,0:T(2,128)S(1)} %add.9), channel_id=1, source_target_pairs={{0,16},{4,20},{8,24},{12,28},{16,0},{20,4},{24,8},{28,12},{1,17},{... | collective-permute-start | bytes 6152 | tf_op jit(solution)/shard_map/ppermute | solution.py:40
  34.0 1.2 collective-permute-start.17
  35.2 2.8 %copy-start = (bf16[2,3,8,64,1024]{4,3,2,1,0:T(8,128)(2,1)S(1)}, bf16[2,3,8,64,1024]{4,3,2,1,0:T(8,128)(2,1)}, u32[]{:S(2)}) copy-start(bf16[2,3,8,64,1024]{4,3,2,1,0:T(8,128)(2,1)} %refs_0_.13) | copy-start | bytes 18874372
  38.5 12.5 %collective-permute-start.27 = (bf16[128,256]{1,0:T(8,128)(2,1)S(1)}, bf16[128,256]{1,0:T(8,128)(2,1)S(1)}, u32[]{:S(2)}, u32[]{:S(2)}) collective-permute-start(bf16[128,256]{1,0:T(8,128)(2,1)S(1)} %get-tuple-element.59), channel_id=1, source_target_pairs={{0,10},{1,11},{2,8},{3,9},{4,14},{5,15},{6,12},{7,13},{8,2},{9,3},... | collective-permute-start | bytes 196616 | tf_op jit(solution)/shard_map/ppermute | solution.py:254
  42.5 9.3 %collective-permute-start.28 = (bf16[128,256]{1,0:T(8,128)(2,1)S(1)}, bf16[128,256]{1,0:T(8,128)(2,1)S(1)}, u32[]{:S(2)}, u32[]{:S(2)}) collective-permute-start(bf16[128,256]{1,0:T(8,128)(2,1)S(1)} %get-tuple-element.60), channel_id=1, source_target_pairs={{0,14},{1,15},{2,12},{3,13},{4,10},{5,11},{6,8},{7,9},{8,6},{9,7},... | collective-permute-start | bytes 196616 | tf_op jit(solution)/shard_map/ppermute | solution.py:254
  42.5 3.9 %collective-permute-start.26 = (bf16[8,256]{1,0:T(8,128)(2,1)S(1)}, bf16[8,256]{1,0:T(8,128)(2,1)S(1)}, u32[]{:S(2)}, u32[]{:S(2)}) collective-permute-start(bf16[8,256]{1,0:T(8,128)(2,1)S(1)} %get-tuple-element.57), channel_id=1, source_target_pairs={{0,1},{1,0},{2,3},{3,2},{4,5},{5,4},{6,7},{7,6},{8,9},{9,8},{10,11... | collective-permute-start | bytes 12296 | tf_op jit(solution)/shard_map/ppermute | solution.py:254
  44.1 14.5 %collective-permute-start.29 = (bf16[128,256]{1,0:T(8,128)(2,1)S(1)}, bf16[128,256]{1,0:T(8,128)(2,1)S(1)}, u32[]{:S(2)}, u32[]{:S(2)}) collective-permute-start(bf16[128,256]{1,0:T(8,128)(2,1)S(1)} %get-tuple-element.61), channel_id=1, source_target_pairs={{0,2},{1,3},{2,0},{3,1},{4,6},{5,7},{6,4},{7,5},{8,10},{9,11},{10,... | collective-permute-start | bytes 196616 | tf_op jit(solution)/shard_map/ppermute | solution.py:254
  46.5 14.3 %collective-permute-start.19 = (bf16[192,256]{1,0:T(8,128)(2,1)S(1)}, bf16[192,256]{1,0:T(8,128)(2,1)S(1)}, u32[]{:S(2)}, u32[]{:S(2)}) collective-permute-start(bf16[192,256]{1,0:T(8,128)(2,1)S(1)} %get-tuple-element.50), channel_id=1, source_target_pairs={{0,7},{1,6},{2,5},{3,4},{4,3},{5,2},{6,1},{7,0},{8,15},{9,14},{10,... | collective-permute-start | bytes 294920 | tf_op jit(solution)/shard_map/ppermute | solution.py:254
  46.5 21.2 %collective-permute-start.20 = (bf16[192,256]{1,0:T(8,128)(2,1)S(1)}, bf16[192,256]{1,0:T(8,128)(2,1)S(1)}, u32[]{:S(2)}, u32[]{:S(2)}) collective-permute-start(bf16[192,256]{1,0:T(8,128)(2,1)S(1)} %get-tuple-element.51), channel_id=1, source_target_pairs={{0,11},{1,10},{2,9},{3,8},{4,15},{5,14},{6,13},{7,12},{8,3},{9,2},... | collective-permute-start | bytes 294920 | tf_op jit(solution)/shard_map/ppermute | solution.py:254
  51.0 17.7 %collective-permute-start.21 = (bf16[192,256]{1,0:T(8,128)(2,1)S(1)}, bf16[192,256]{1,0:T(8,128)(2,1)S(1)}, u32[]{:S(2)}, u32[]{:S(2)}) collective-permute-start(bf16[192,256]{1,0:T(8,128)(2,1)S(1)} %get-tuple-element.52), channel_id=1, source_target_pairs={{0,15},{1,14},{2,13},{3,12},{4,11},{5,10},{6,9},{7,8},{8,7},{9,6},... | collective-permute-start | bytes 294920 | tf_op jit(solution)/shard_map/ppermute | solution.py:254
  51.9 31.1 %collective-permute-start.23 = (bf16[192,256]{1,0:T(8,128)(2,1)S(1)}, bf16[192,256]{1,0:T(8,128)(2,1)S(1)}, u32[]{:S(2)}, u32[]{:S(2)}) collective-permute-start(bf16[192,256]{1,0:T(8,128)(2,1)S(1)} %get-tuple-element.54), channel_id=1, source_target_pairs={{0,6},{1,7},{2,4},{3,5},{4,2},{5,3},{6,0},{7,1},{8,14},{9,15},{10,... | collective-permute-start | bytes 294920 | tf_op jit(solution)/shard_map/ppermute | solution.py:254
  58.6 27.5 %collective-permute-start.24 = (bf16[192,256]{1,0:T(8,128)(2,1)S(1)}, bf16[192,256]{1,0:T(8,128)(2,1)S(1)}, u32[]{:S(2)}, u32[]{:S(2)}) collective-permute-start(bf16[192,256]{1,0:T(8,128)(2,1)S(1)} %get-tuple-element.55), channel_id=1, source_target_pairs={{0,10},{1,11},{2,8},{3,9},{4,14},{5,15},{6,12},{7,13},{8,2},{9,3},... | collective-permute-start | bytes 294920 | tf_op jit(solution)/shard_map/ppermute | solution.py:254
  60.8 54.1 %collective-permute-start.1 = (bf16[448,256]{1,0:T(8,128)(2,1)}, bf16[448,256]{1,0:T(8,128)(2,1)S(1)}, u32[]{:S(2)}, u32[]{:S(2)}) collective-permute-start(bf16[448,256]{1,0:T(8,128)(2,1)} %get-tuple-element.35), channel_id=1, source_target_pairs={{0,7},{1,6},{2,5},{3,4},{4,3},{5,2},{6,1},{7,0},{8,15},{9,14},{10,... | collective-permute-start | bytes 688136 | tf_op jit(solution)/shard_map/ppermute | solution.py:254
  67.7 51.2 %collective-permute-start.2 = (bf16[448,256]{1,0:T(8,128)(2,1)}, bf16[448,256]{1,0:T(8,128)(2,1)S(1)}, u32[]{:S(2)}, u32[]{:S(2)}) collective-permute-start(bf16[448,256]{1,0:T(8,128)(2,1)} %get-tuple-element.36), channel_id=1, source_target_pairs={{0,11},{1,10},{2,9},{3,8},{4,15},{5,14},{6,13},{7,12},{8,3},{9,2},... | collective-permute-start | bytes 688136 | tf_op jit(solution)/shard_map/ppermute | solution.py:254
  68.7 43.2 %collective-permute-start.18 = (bf16[200,256]{1,0:T(8,128)(2,1)S(1)}, bf16[200,256]{1,0:T(8,128)(2,1)S(1)}, u32[]{:S(2)}, u32[]{:S(2)}) collective-permute-start(bf16[200,256]{1,0:T(8,128)(2,1)S(1)} %get-tuple-element.49), channel_id=1, source_target_pairs={{0,3},{1,2},{2,1},{3,0},{4,7},{5,6},{6,5},{7,4},{8,11},{9,10},{10,... | collective-permute-start | bytes 307208 | tf_op jit(solution)/shard_map/ppermute | solution.py:254
  83.0 29.4 %collective-permute-start.22 = (bf16[200,256]{1,0:T(8,128)(2,1)S(1)}, bf16[200,256]{1,0:T(8,128)(2,1)S(1)}, u32[]{:S(2)}, u32[]{:S(2)}) collective-permute-start(bf16[200,256]{1,0:T(8,128)(2,1)S(1)} %get-tuple-element.53), channel_id=1, source_target_pairs={{0,2},{1,3},{2,0},{3,1},{4,6},{5,7},{6,4},{7,5},{8,10},{9,11},{10,... | collective-permute-start | bytes 307208 | tf_op jit(solution)/shard_map/ppermute | solution.py:254
  86.1 20.5 %collective-permute-start.25 = (bf16[192,256]{1,0:T(8,128)(2,1)S(1)}, bf16[192,256]{1,0:T(8,128)(2,1)S(1)}, u32[]{:S(2)}, u32[]{:S(2)}) collective-permute-start(bf16[192,256]{1,0:T(8,128)(2,1)S(1)} %get-tuple-element.56), channel_id=1, source_target_pairs={{0,14},{1,15},{2,12},{3,13},{4,10},{5,11},{6,8},{7,9},{8,6},{9,7},... | collective-permute-start | bytes 294920 | tf_op jit(solution)/shard_map/ppermute | solution.py:254
  106.6 12.3 %collective-permute-start.3 = (bf16[448,256]{1,0:T(8,128)(2,1)}, bf16[448,256]{1,0:T(8,128)(2,1)S(1)}, u32[]{:S(2)}, u32[]{:S(2)}) collective-permute-start(bf16[448,256]{1,0:T(8,128)(2,1)} %get-tuple-element.37), channel_id=1, source_target_pairs={{0,15},{1,14},{2,13},{3,12},{4,11},{5,10},{6,9},{7,8},{8,7},{9,6},... | collective-permute-start | bytes 688136 | tf_op jit(solution)/shard_map/ppermute | solution.py:254
  111.9 18.0 %collective-permute-start = (bf16[448,256]{1,0:T(8,128)(2,1)}, bf16[448,256]{1,0:T(8,128)(2,1)S(1)}, u32[]{:S(2)}, u32[]{:S(2)}) collective-permute-start(bf16[448,256]{1,0:T(8,128)(2,1)} %pack.8), channel_id=1, source_target_pairs={{0,3},{1,2},{2,1},{3,0},{4,7},{5,6},{6,5},{7,4},{8,11},{9,10},{10,... | collective-permute-start | bytes 688136 | tf_op jit(solution)/shard_map/ppermute | solution.py:254
  112.3 27.4 %collective-permute-start.10 = (bf16[448,256]{1,0:T(8,128)(2,1)}, bf16[448,256]{1,0:T(8,128)(2,1)S(1)}, u32[]{:S(2)}, u32[]{:S(2)}) collective-permute-start(bf16[448,256]{1,0:T(8,128)(2,1)} %get-tuple-element.44), channel_id=1, source_target_pairs={{0,10},{1,11},{2,8},{3,9},{4,14},{5,15},{6,12},{7,13},{8,2},{9,3},... | collective-permute-start | bytes 688136 | tf_op jit(solution)/shard_map/ppermute | solution.py:254
  114.9 53.2 %collective-permute-start.4 = (bf16[768,256]{1,0:T(8,128)(2,1)}, bf16[768,256]{1,0:T(8,128)(2,1)S(1)}, u32[]{:S(2)}, u32[]{:S(2)}) collective-permute-start(bf16[768,256]{1,0:T(8,128)(2,1)} %get-tuple-element.38), channel_id=1, source_target_pairs={{0,1},{1,0},{2,3},{3,2},{4,5},{5,4},{6,7},{7,6},{8,9},{9,8},{10,11... | collective-permute-start | bytes 1179656 | tf_op jit(solution)/shard_map/ppermute | solution.py:254
  118.9 50.8 %collective-permute-start.5 = (bf16[768,256]{1,0:T(8,128)(2,1)}, bf16[768,256]{1,0:T(8,128)(2,1)S(1)}, u32[]{:S(2)}, u32[]{:S(2)}) collective-permute-start(bf16[768,256]{1,0:T(8,128)(2,1)} %get-tuple-element.39), channel_id=1, source_target_pairs={{0,5},{1,4},{2,7},{3,6},{4,1},{5,0},{6,3},{7,2},{8,13},{9,12},{10,... | collective-permute-start | bytes 1179656 | tf_op jit(solution)/shard_map/ppermute | solution.py:254
  118.9 28.9 %collective-permute-start.11 = (bf16[448,256]{1,0:T(8,128)(2,1)}, bf16[448,256]{1,0:T(8,128)(2,1)S(1)}, u32[]{:S(2)}, u32[]{:S(2)}) collective-permute-start(bf16[448,256]{1,0:T(8,128)(2,1)} %get-tuple-element.45), channel_id=1, source_target_pairs={{0,14},{1,15},{2,12},{3,13},{4,10},{5,11},{6,8},{7,9},{8,6},{9,7},... | collective-permute-start | bytes 688136 | tf_op jit(solution)/shard_map/ppermute | solution.py:254
  129.9 33.5 %collective-permute-start.8 = (bf16[448,256]{1,0:T(8,128)(2,1)}, bf16[448,256]{1,0:T(8,128)(2,1)S(1)}, u32[]{:S(2)}, u32[]{:S(2)}) collective-permute-start(bf16[448,256]{1,0:T(8,128)(2,1)} %get-tuple-element.42), channel_id=1, source_target_pairs={{0,2},{1,3},{2,0},{3,1},{4,6},{5,7},{6,4},{7,5},{8,10},{9,11},{10,... | collective-permute-start | bytes 688136 | tf_op jit(solution)/shard_map/ppermute | solution.py:254
  139.8 28.2 %collective-permute-start.9 = (bf16[448,256]{1,0:T(8,128)(2,1)}, bf16[448,256]{1,0:T(8,128)(2,1)S(1)}, u32[]{:S(2)}, u32[]{:S(2)}) collective-permute-start(bf16[448,256]{1,0:T(8,128)(2,1)} %get-tuple-element.43), channel_id=1, source_target_pairs={{0,6},{1,7},{2,4},{3,5},{4,2},{5,3},{6,0},{7,1},{8,14},{9,15},{10,... | collective-permute-start | bytes 688136 | tf_op jit(solution)/shard_map/ppermute | solution.py:254
  147.8 22.0 %collective-permute-start.6 = (bf16[768,256]{1,0:T(8,128)(2,1)}, bf16[768,256]{1,0:T(8,128)(2,1)S(1)}, u32[]{:S(2)}, u32[]{:S(2)}) collective-permute-start(bf16[768,256]{1,0:T(8,128)(2,1)} %get-tuple-element.40), channel_id=1, source_target_pairs={{0,9},{1,8},{2,11},{3,10},{4,13},{5,12},{6,15},{7,14},{8,1},{9,0},... | collective-permute-start | bytes 1179656 | tf_op jit(solution)/shard_map/ppermute | solution.py:254
  163.4 19.8 %collective-permute-start.7 = (bf16[768,256]{1,0:T(8,128)(2,1)}, bf16[768,256]{1,0:T(8,128)(2,1)S(1)}, u32[]{:S(2)}, u32[]{:S(2)}) collective-permute-start(bf16[768,256]{1,0:T(8,128)(2,1)} %get-tuple-element.41), channel_id=1, source_target_pairs={{0,13},{1,12},{2,15},{3,14},{4,9},{5,8},{6,11},{7,10},{8,5},{9,4},... | collective-permute-start | bytes 1179656 | tf_op jit(solution)/shard_map/ppermute | solution.py:254
  168.0 15.3 %collective-permute-start.12 = (bf16[768,256]{1,0:T(8,128)(2,1)}, bf16[768,256]{1,0:T(8,128)(2,1)S(1)}, u32[]{:S(2)}, u32[]{:S(2)}) collective-permute-start(bf16[768,256]{1,0:T(8,128)(2,1)} %get-tuple-element.46), channel_id=1, source_target_pairs={{0,4},{1,5},{2,6},{3,7},{4,0},{5,1},{6,2},{7,3},{8,12},{9,13},{10,... | collective-permute-start | bytes 1179656 | tf_op jit(solution)/shard_map/ppermute | solution.py:254
  168.0 24.9 %collective-permute-start.13 = (bf16[768,256]{1,0:T(8,128)(2,1)}, bf16[768,256]{1,0:T(8,128)(2,1)S(1)}, u32[]{:S(2)}, u32[]{:S(2)}) collective-permute-start(bf16[768,256]{1,0:T(8,128)(2,1)} %get-tuple-element.47), channel_id=1, source_target_pairs={{0,8},{1,9},{2,10},{3,11},{4,12},{5,13},{6,14},{7,15},{8,0},{9,1},... | collective-permute-start | bytes 1179656 | tf_op jit(solution)/shard_map/ppermute | solution.py:254
  169.7 31.5 %collective-permute-start.14 = (bf16[768,256]{1,0:T(8,128)(2,1)}, bf16[768,256]{1,0:T(8,128)(2,1)S(1)}, u32[]{:S(2)}, u32[]{:S(2)}) collective-permute-start(bf16[768,256]{1,0:T(8,128)(2,1)} %get-tuple-element.48), channel_id=1, source_target_pairs={{0,12},{1,13},{2,14},{3,15},{4,8},{5,9},{6,10},{7,11},{8,4},{9,5},... | collective-permute-start | bytes 1179656 | tf_op jit(solution)/shard_map/ppermute | solution.py:254
  169.8 43.3 %collective-permute-start.30 = (bf16[128,256]{1,0:T(8,128)(2,1)S(1)}, bf16[128,256]{1,0:T(8,128)(2,1)S(1)}, u32[]{:S(2)}, u32[]{:S(2)}) collective-permute-start(bf16[128,256]{1,0:T(8,128)(2,1)S(1)} %get-tuple-element.62), channel_id=1, source_target_pairs={{0,6},{1,7},{2,4},{3,5},{4,2},{5,3},{6,0},{7,1},{8,14},{9,15},{10,... | collective-permute-start | bytes 196616 | tf_op jit(solution)/shard_map/ppermute | solution.py:254
  183.2 30.8 %collective-permute-start.31 = (bf16[128,256]{1,0:T(8,128)(2,1)S(1)}, bf16[128,256]{1,0:T(8,128)(2,1)S(1)}, u32[]{:S(2)}, u32[]{:S(2)}) collective-permute-start(bf16[128,256]{1,0:T(8,128)(2,1)S(1)} %get-tuple-element.63), channel_id=1, source_target_pairs={{0,11},{1,10},{2,9},{3,8},{4,15},{5,14},{6,13},{7,12},{8,3},{9,2},... | collective-permute-start | bytes 196616 | tf_op jit(solution)/shard_map/ppermute | solution.py:254
  183.2 30.8 %collective-permute-start.32 = (bf16[128,256]{1,0:T(8,128)(2,1)S(1)}, bf16[128,256]{1,0:T(8,128)(2,1)S(1)}, u32[]{:S(2)}, u32[]{:S(2)}) collective-permute-start(bf16[128,256]{1,0:T(8,128)(2,1)S(1)} %get-tuple-element.64), channel_id=1, source_target_pairs={{0,15},{1,14},{2,13},{3,12},{4,11},{5,10},{6,9},{7,8},{8,7},{9,6},... | collective-permute-start | bytes 196616 | tf_op jit(solution)/shard_map/ppermute | solution.py:254
  192.9 21.9 %collective-permute-start.33 = (bf16[128,256]{1,0:T(8,128)(2,1)S(1)}, bf16[128,256]{1,0:T(8,128)(2,1)S(1)}, u32[]{:S(2)}, u32[]{:S(2)}) collective-permute-start(bf16[128,256]{1,0:T(8,128)(2,1)S(1)} %get-tuple-element.65), channel_id=1, source_target_pairs={{0,3},{1,2},{2,1},{3,0},{4,7},{5,6},{6,5},{7,4},{8,11},{9,10},{10,... | collective-permute-start | bytes 196616 | tf_op jit(solution)/shard_map/ppermute | solution.py:254
  201.3 13.5 %collective-permute-start.34 = (bf16[128,256]{1,0:T(8,128)(2,1)S(1)}, bf16[128,256]{1,0:T(8,128)(2,1)S(1)}, u32[]{:S(2)}, u32[]{:S(2)}) collective-permute-start(bf16[128,256]{1,0:T(8,128)(2,1)S(1)} %get-tuple-element.66), channel_id=1, source_target_pairs={{0,7},{1,6},{2,5},{3,4},{4,3},{5,2},{6,1},{7,0},{8,15},{9,14},{10,... | collective-permute-start | bytes 196616 | tf_op jit(solution)/shard_map/ppermute | solution.py:254
  203.1 1.0 copy-start.1
